TPU v7x, 128 devices: a whole 4x4x4 slice. The times are simulated.
128 devices in a mesh: depth: 8 (over y, core), lat: 16 (over z, x).
Axes of the slice: x: 4, y: 4, z: 4, core: 2. Of those that a mesh axis runs over, the one named last changes fastest.
Arguments:
- emission: float32 [1024, 16, 2048], P('depth', None, 'lat'), may hold values from 0 to 2
- absorption: float32 [1024, 16, 2048], P('depth', None, 'lat'), may hold values from -4 to 4
- target: float32 [3, 16, 2048], P(None, None, 'lat'), may hold values from 0.2 to 0.8
- shift_whole: int32 [3, 1024], P(None, 'depth'), may hold values from -30 to 30, as said below
- shift_fraction: int32 [3, 1024], P(None, 'depth'), may hold values from 0 to 7, as said below
- taps_table: float32 [8, 4], replicated, may hold values from 0.05 to 0.45
Outputs:
- fitted_emission: float32 [1024, 16, 2048], P('depth', None, 'lat')
- fitted_absorption: float32 [1024, 16, 2048], P('depth', None, 'lat')
Inputs may be any that keep to these rules, and one draw needn't show every extreme that they name: `shift_whole`: both ends of the range are taken in every draw. `shift_fraction`: every value of the range is taken in every draw.
All inputs are finite; a program needn't handle non-finite values.
Results may differ from a plain program's by a relative error of at most 0.0003.
Values sent between devices are 32-bit elements; how exact they have to be, the bound alone decides.
No kernel may reach another device: no remote copies, remote signals or barrier semaphores. Data moves between devices by JAX's collectives and lax.ppermute only.
A program may use at most 128 MiB of HBM per device.

v0:
```python
import jax
import jax.numpy as jnp
from jax import lax
from jax.sharding import PartitionSpec as P

REACH = 32
ITERS = 3


HIGHEST = lax.Precision.HIGHEST
LEARN_RATE = 0.1
BETA_FIRST = 0.9
BETA_SECOND = 0.999
ADAM_EPSILON = 0.001


def copy_for_each(x, axis):
    devices = lax.axis_size(axis)
    return lax.all_to_all(jnp.broadcast_to(x[None], (devices, *x.shape)), axis, 0, 0, tiled=True)


def all_in_one(x, axis):
    leaves = jax.tree.leaves(x)
    sequence = sorted(range(len(leaves)), key=lambda k: -leaves[k].size)
    width = (1, *leaves[sequence[0]].shape)[-1]
    lines = [
        jnp.pad(leaves[k].reshape(-1), (0, -leaves[k].size % width)).reshape(-1, width)
        for k in sequence
    ]
    both, at, found = (copy_for_each(jnp.concatenate(lines), axis), 0, {})
    for k, line in zip(sequence, lines):
        slab = both[:, at : at + len(line)].reshape(len(both), -1)
        found[k] = slab[:, : leaves[k].size].reshape(-1, *leaves[k].shape)
        at += len(line)
    numbers = iter(range(len(leaves)))
    return jax.tree.map(lambda _: found[next(numbers)], x)


def once_a_type(x, axis):
    leaves, found = (jax.tree.leaves(x), {})
    for leading, a in enumerate(leaves):
        if leading not in found:
            alike = [k for k, b in enumerate(leaves) if b.dtype == a.dtype]
            got = (
                all_in_one([leaves[k] for k in alike], axis)
                if len(alike) > 1
                else [copy_for_each(a, axis)]
            )
            for k, b in zip(alike, got):
                found[k] = b
    numbers = iter(range(len(leaves)))
    return jax.tree.map(lambda _: found[next(numbers)], x)


def combined_pairwise(pieces, combine):
    while len(jax.tree.leaves(pieces)[0]) > 1:
        pieces = jax.vmap(combine)(
            *(jax.tree.map(lambda part: part[side::2], pieces) for side in (0, 1))
        )
    return jax.tree.map(lambda part: part[0], pieces)


def carried_in(x, axis, combine, identity, reverse):
    devices, here = (lax.axis_size(axis), lax.axis_index(axis))
    passed = jnp.arange(devices) > here if reverse else jnp.arange(devices) < here

    def kept(part, zero, own):
        part = jnp.where(
            passed.reshape(-1, *(1 for _ in own.shape)), part, jnp.asarray(zero, own.dtype)
        )
        return part[::-1] if reverse else part

    pieces = once_a_type(x, axis)
    return combined_pairwise(jax.tree.map(kept, pieces, identity, x), combine)


def plane_taps(fractions, taps_table):
    levels = jnp.arange(taps_table.shape[0], dtype=jnp.int32)
    picks = (fractions[:, None] == levels[None, :]).astype(jnp.float32)
    return jnp.dot(picks, taps_table, precision=HIGHEST)


def build_band(offsets, tap_weights, tile_width):
    source = jnp.arange(tile_width + 2 * REACH, dtype=jnp.int32)[None, :, None]
    column = jnp.arange(tile_width, dtype=jnp.int32)[None, None, :]
    lag_taps = source - column - REACH - offsets[:, None, None] + 1
    banded = jnp.zeros((offsets.shape[0], tile_width + 2 * REACH, tile_width), jnp.float32)
    for tap_index in range(tap_weights.shape[1]):
        banded = banded + jnp.where(
            lag_taps == tap_index, tap_weights[:, tap_index][:, None, None], 0.0
        )
    return banded


def combine_front(earlier, later):
    return (earlier[0] + jnp.exp(-earlier[1]) * later[0], earlier[1] + later[1])


def combine_back(earlier, later):
    return (later[0] + jnp.exp(-later[1]) * earlier[0], earlier[1] + later[1])


def with_margins(fields):
    blank = jnp.zeros(fields.shape[:3] + (1, REACH), jnp.float32)
    left_part = jnp.concatenate([blank, fields[:, :, :, :-1, -REACH:]], axis=3)
    right_part = jnp.concatenate([fields[:, :, :, 1:, :REACH], blank], axis=3)
    widened = jnp.concatenate([left_part, fields, right_part], axis=4)
    return widened


def fold_margins(spread, tile_width):
    left_rim = spread[:, :, :, :, :REACH]
    right_rim = spread[:, :, :, :, tile_width + REACH :]
    centre = spread[:, :, :, :, REACH : tile_width + REACH]
    blank = jnp.zeros(left_rim.shape[:3] + (1, REACH), jnp.float32)
    from_right = jnp.concatenate([left_rim[:, :, :, 1:], blank], axis=3)
    from_left = jnp.concatenate([blank, right_rim[:, :, :, :-1]], axis=3)
    spacing = ((0, 0), (0, 0), (0, 0), (0, 0))
    tail_part = jnp.pad(from_right, spacing + ((tile_width - REACH, 0),))
    head_part = jnp.pad(from_left, spacing + ((0, tile_width - REACH),))
    return centre + head_part + tail_part


def body(emission, absorption, target, shift_whole, shift_fraction, taps_table):
    tile_width = emission.shape[2]
    total_planes = emission.shape[0] * lax.axis_size("depth")
    fields = jnp.stack([emission, absorption])
    tile_count = lax.axis_size("lat")
    fields, goals = (
        lax.all_to_all(fields, "lat", split_axis=2, concat_axis=3, tiled=True),
        lax.all_to_all(target[None], "lat", split_axis=2, concat_axis=3, tiled=True),
    )
    fields = fields.reshape(fields.shape[:3] + (tile_count, tile_width))
    goals = goals[0].reshape(goals.shape[1:3] + (tile_count, tile_width))
    first_moment = jnp.zeros_like(fields)
    second_moment = jnp.zeros_like(fields)
    for view_index in range(ITERS):
        tap_weights = plane_taps(shift_fraction[view_index], taps_table)
        banded = build_band(shift_whole[view_index], tap_weights, tile_width)
        sheared = jnp.einsum("czrtj,zjx->czrtx", with_margins(fields), banded, precision=HIGHEST)
        color_raw = sheared[0]
        density = sheared[1]
        optical = jax.nn.softplus(density) / total_planes
        transmit_local = jnp.exp(optical - jnp.cumsum(optical, axis=0))
        opacity = -jnp.expm1(-optical)
        emitted = transmit_local * opacity * color_raw
        slab_light = jnp.sum(emitted, axis=0)
        slab_depth = jnp.sum(optical, axis=0)
        blank = jnp.zeros_like(slab_light)
        front_light, front_depth = carried_in(
            (slab_light, slab_depth), "depth", combine_front, (blank, blank), False
        )
        attenuate = jnp.exp(-front_depth)
        back_light, back_depth = carried_in(
            (slab_light, slab_depth), "depth", combine_back, (blank, blank), True
        )
        rendered = front_light + attenuate * (slab_light + jnp.exp(-slab_depth) * back_light)
        residual = rendered - goals[view_index]
        transmit = attenuate * transmit_local
        behind = rendered - front_light - attenuate * jnp.cumsum(emitted, axis=0)
        grad_color = total_planes * residual * transmit * opacity
        grad_density = (
            residual * (transmit * jnp.exp(-optical) * color_raw - behind) * jax.nn.sigmoid(density)
        )
        spread = jnp.einsum(
            "czrtx,zjx->czrtj", jnp.stack([grad_color, grad_density]), banded, precision=HIGHEST
        )
        gradient = fold_margins(spread, tile_width)
        step_number = view_index + 1
        first_moment = BETA_FIRST * first_moment + (1.0 - BETA_FIRST) * gradient
        second_moment = BETA_SECOND * second_moment + (1.0 - BETA_SECOND) * gradient * gradient
        scaled_first = first_moment / (1.0 - BETA_FIRST**step_number)
        scaled_second = second_moment / (1.0 - BETA_SECOND**step_number)
        fields = fields - LEARN_RATE * scaled_first / (jnp.sqrt(scaled_second) + ADAM_EPSILON)
    fields = fields.reshape(fields.shape[:3] + (fields.shape[3] * tile_width,))
    fields = lax.all_to_all(fields, "lat", split_axis=3, concat_axis=2, tiled=True)
    return (fields[0], fields[1])


def solution(mesh):
    in_specs = (
        P("depth", None, "lat"),
        P("depth", None, "lat"),
        P(None, None, "lat"),
        P(None, "depth"),
        P(None, "depth"),
        P(),
    )
    out_specs = (P("depth", None, "lat"), P("depth", None, "lat"))
    return jax.shard_map(body, mesh=mesh, in_specs=in_specs, out_specs=out_specs, check_vma=False)
```

profile of v0, /device:TPU:0, one launch (start us, length us, event | category | flops | bytes accessed | tf_op | source)
XLA Modules:
  0.0 288.7 jit_solution(7464354828743110071)
XLA Ops:
  0.6 1.6 copy.199
  2.2 1.6 copy.200
  3.8 3.2 %pad_maximum_fusion = f32[2,128,16,128]{3,0,1,2:T(2,128)} fusion(f32[1,128,16,128]{3,0,1,2:T(1,128)S(1)} %bitcast.608, f32[1,128,16,128]{3,0,1,2:T(1,128)S(1)} %bitcast.607), kind=kLoop, calls=%fused_computation.74 | loop fusion | flops 524288 | bytes 4194304 | tf_op jit(solution)/shard_map/stack | solution.py:127
  7.0 8.1 %all-to-all-start = ((f32[2,128,16,128]{3,0,1,2:T(2,128)}), f32[2,128,16,128]{3,0,1,2:T(2,128)S(1)}, u32[]{:S(2)}, u32[]{:S(2)}) async-start(f32[2,128,16,128]{3,0,1,2:T(2,128)} %pad_maximum_fusion), calls=%async_computation | async-start | bytes 4194304 | tf_op jit(solution)/shard_map/all_to_all | solution.py:130
  15.2 0.6 copy.206
  16.3 0.3 fusion.167
  16.6 30.3 %all-to-all-done = f32[2,128,16,128]{3,0,1,2:T(2,128)S(1)} async-done(((f32[2,128,16,128]{3,0,1,2:T(2,128)}), f32[2,128,16,128]{3,0,1,2:T(2,128)S(1)}, u32[]{:S(2)}, u32[]{:S(2)}) %all-to-all-start) | async-done | bytes 2097184 | tf_op jit(solution)/shard_map/all_to_all | solution.py:130
  46.9 3.7 %all-to-all-start.2 = ((f32[1,3,16,128]{3,0,1,2:T(1,128)}), f32[1,3,16,128]{3,0,1,2:T(1,128)S(1)}, u32[]{:S(2)}, u32[]{:S(2)}) async-start(f32[1,3,16,128]{3,0,1,2:T(1,128)} %copy.206), calls=%async_computation.2 | async-start | bytes 49152 | tf_op jit(solution)/shard_map/all_to_all | solution.py:131
  50.6 1.2 copy.280
  51.8 0.8 fusion.268
  52.6 17.9 %fusion.58 = f32[2,128,1,16,128]{4,3,0,1,2:T(8,128)S(1)} fusion(f32[2,128,1,15,32]{4,3,0,1,2:T(8,128)S(1)} %get-tuple-element.37, f32[2,128,1,15,32]{4,3,0,1,2:T(8,128)S(1)} %get-tuple-element.36, f32[2,128,1,16,128]{4,3,0,1,2:T(8,128)S(1)} %bitcast.603, f32[128]{0:T(128)S(1)} %get-tuple-element.115, f32[128]{0:T(128)S(1)} %get-tuple-element.116, ...), kind=kOutput, calls=%fused_computation.91 | convolution fusion | flops 1253572608 | bytes 5278208 | tf_op jit(solution)/shard_map/czrtj,zjx->czrtx/dot_general | solution.py:140
  70.5 1.2 fusion.141
  71.7 0.7 broadcast_in_dim.227
  72.4 4.5 %all-to-all-start.1 = ((f32[8,32,128]{2,1,0:T(8,128)}), f32[8,32,128]{2,1,0:T(8,128)S(1)}, u32[]{:S(2)}, u32[]{:S(2)}) async-start(f32[8,32,128]{2,1,0:T(8,128)} %broadcast_in_dim.227), calls=%async_computation.1 | async-start | bytes 262144 | tf_op jit(solution)/shard_map/all_to_all | solution.py:19
  76.9 6.1 %all-to-all-done.1 = f32[8,32,128]{2,1,0:T(8,128)S(1)} async-done(((f32[8,32,128]{2,1,0:T(8,128)}), f32[8,32,128]{2,1,0:T(8,128)S(1)}, u32[]{:S(2)}, u32[]{:S(2)}) %all-to-all-start.1) | async-done | bytes 131104 | tf_op jit(solution)/shard_map/all_to_all | solution.py:19
  83.2 1.1 bitcast_multiply_fusion.11
  84.4 1.5 fusion.106
  85.9 26.7 %fusion.33 = f32[2,128,1,16,192]{4,3,0,1,2:T(8,128)S(1)} fusion(f32[128]{0:T(128)S(1)} %get-tuple-element.115, f32[128]{0:T(128)S(1)} %get-tuple-element.116, f32[128]{0:T(128)S(1)} %get-tuple-element.117, f32[128]{0:T(128)S(1)} %get-tuple-element.114, s32[128]{0:T(128)S(1)} %get-tuple-element.101, s32[192,128]{1,0:T(8,128)S(1)} %subtract_add_fusion.3, ...), kind=kOutput, calls=%fused_computation.55 | convolution fusion | flops 1249378304 | bytes 5343744 | tf_op jit(solution)/shard_map/czrtx,zjx->czrtj/dot_general | solution.py:165
  112.6 0.8 fusion.264
  113.5 0.7 copy-done.3
  114.2 3.8 %divide_subtract_fusion.1 = (f32[2,128,1,16,128]{4,3,0,1,2:T(8,128)S(1)}, f32[2,128,1,16,128]{4,3,0,1,2:T(8,128)}) fusion(f32[2,128,16,128]{3,0,1,2:T(2,128)S(1)} %copy-done.3, f32[2,128,1,15,32]{4,3,0,1,2:T(8,128)S(1)} %get-tuple-element.29, f32[2,128,1,15,32]{4,3,0,1,2:T(8,128)S(1)} %get-tuple-element.28, f32[2,128,1,16,192]{4,3,0,1,2:T(8,128)S(1)} %fusion.33), kind=kLoop, calls=%fused_computation.90 | loop fusion | flops 4718592 | bytes 9371648 | tf_op jit(solution)/shard_map/sub | solution.py:174
  118.0 0.8 fusion.267
  118.8 17.5 %fusion.63 = f32[2,128,1,16,128]{4,3,1,2,0:T(8,128)S(1)} fusion(f32[128]{0:T(128)S(1)} %get-tuple-element.111, f32[128]{0:T(128)S(1)} %get-tuple-element.112, f32[128]{0:T(128)S(1)} %get-tuple-element.113, f32[128]{0:T(128)S(1)} %get-tuple-element.110, s32[128]{0:T(128)S(1)} %get-tuple-element.102, s32[192,128]{1,0:T(8,128)S(1)} %subtract_add_fusion.3, ...), kind=kOutput, calls=%fused_computation.92 | convolution fusion | flops 1253572608 | bytes 5278208 | tf_op jit(solution)/shard_map/czrtj,zjx->czrtx/dot_general | solution.py:140
  136.3 1.2 fusion.92
  137.5 0.7 broadcast_in_dim.239
  138.2 3.4 %all-to-all-start.3 = ((f32[8,32,128]{2,1,0:T(8,128)}), f32[8,32,128]{2,1,0:T(8,128)S(1)}, u32[]{:S(2)}, u32[]{:S(2)}) async-start(f32[8,32,128]{2,1,0:T(8,128)} %broadcast_in_dim.239), calls=%async_computation.3 | async-start | bytes 262144 | tf_op jit(solution)/shard_map/all_to_all | solution.py:19
  141.6 6.0 %all-to-all-done.3 = f32[8,32,128]{2,1,0:T(8,128)S(1)} async-done(((f32[8,32,128]{2,1,0:T(8,128)}), f32[8,32,128]{2,1,0:T(8,128)S(1)}, u32[]{:S(2)}, u32[]{:S(2)}) %all-to-all-start.3) | async-done | bytes 131104 | tf_op jit(solution)/shard_map/all_to_all | solution.py:19
  147.8 1.1 fusion.153
  149.0 1.5 fusion.74
  150.5 26.8 %fusion.36 = f32[2,128,1,16,192]{4,3,0,1,2:T(8,128)S(1)} fusion(f32[128]{0:T(128)S(1)} %get-tuple-element.111, f32[128]{0:T(128)S(1)} %get-tuple-element.112, f32[128]{0:T(128)S(1)} %get-tuple-element.113, f32[128]{0:T(128)S(1)} %get-tuple-element.110, s32[128]{0:T(128)S(1)} %get-tuple-element.102, s32[192,128]{1,0:T(8,128)S(1)} %subtract_add_fusion.3, ...), kind=kOutput, calls=%fused_computation.56 | convolution fusion | flops 1249378304 | bytes 5343744 | tf_op jit(solution)/shard_map/czrtx,zjx->czrtj/dot_general | solution.py:165
  177.4 0.8 fusion.263
  178.2 0.7 copy-done.4
  178.9 0.6 copy-done.5
  179.6 4.6 %divide_subtract_fusion = f32[2,128,1,16,128]{4,3,0,1,2:T(8,128)S(1)} fusion(f32[2,128,1,16,128]{4,3,0,1,2:T(8,128)S(1)} %copy-done.5, f32[2,128,1,15,32]{4,3,0,1,2:T(8,128)S(1)} %get-tuple-element.27, f32[2,128,1,15,32]{4,3,0,1,2:T(8,128)S(1)} %get-tuple-element.26, f32[2,128,1,16,192]{4,3,0,1,2:T(8,128)S(1)} %fusion.36, f32[2,128,16,128]{3,0,1,2:T(2,128)S(1)} %copy-done.4), kind=kLoop, calls=%fused_computation.88 | loop fusion | flops 11010048 | bytes 9371648 | tf_op jit(solution)/shard_map/sub | solution.py:174
  184.2 0.8 fusion.266
  185.0 17.5 %fusion.68 = f32[2,128,1,16,128]{4,3,1,2,0:T(8,128)S(1)} fusion(f32[128]{0:T(128)S(1)} %get-tuple-element.104, f32[128]{0:T(128)S(1)} %get-tuple-element.105, f32[128]{0:T(128)S(1)} %get-tuple-element.106, f32[128]{0:T(128)S(1)} %get-tuple-element.103, s32[128]{0:T(128)S(1)} %get-tuple-element.100, s32[192,128]{1,0:T(8,128)S(1)} %subtract_add_fusion.3, ...), kind=kOutput, calls=%fused_computation.93 | convolution fusion | flops 1253572608 | bytes 5278208 | tf_op jit(solution)/shard_map/czrtj,zjx->czrtx/dot_general | solution.py:140
  202.5 1.2 fusion.86
  203.7 8.7 %all_to_all.48 = f32[8,32,128]{2,1,0:T(8,128)S(1)} all-to-all(f32[8,32,128]{2,1,0:T(8,128)S(1)} %broadcast_in_dim.248), channel_id=1, replica_groups=mesh['depth'=8,'lat'=16] {'depth'}, dimensions={0} | all-to-all | bytes 262144 | tf_op jit(solution)/shard_map/all_to_all | solution.py:19
  212.6 1.1 fusion.149
  213.8 1.5 fusion.77
  215.3 26.5 %fusion.39 = f32[2,128,1,16,192]{4,3,0,1,2:T(8,128)S(1)} fusion(f32[128]{0:T(128)S(1)} %get-tuple-element.104, f32[128]{0:T(128)S(1)} %get-tuple-element.105, f32[128]{0:T(128)S(1)} %get-tuple-element.106, f32[128]{0:T(128)S(1)} %get-tuple-element.103, s32[128]{0:T(128)S(1)} %get-tuple-element.100, s32[192,128]{1,0:T(8,128)S(1)} %subtract_add_fusion.3, ...), kind=kOutput, calls=%fused_computation.57 | convolution fusion | flops 1249378304 | bytes 5343744 | tf_op jit(solution)/shard_map/czrtx,zjx->czrtj/dot_general | solution.py:165
  241.8 0.8 fusion.262
  242.6 4.0 %fusion.48 = f32[2,128,1,16,128]{4,3,0,1,2:T(8,128)S(1)} fusion(f32[2,128,1,16,128]{4,3,0,1,2:T(8,128)S(1)} %divide_subtract_fusion, f32[2,128,1,15,32]{4,3,0,1,2:T(8,128)S(1)} %get-tuple-element.25, f32[2,128,1,15,32]{4,3,0,1,2:T(8,128)S(1)} %get-tuple-element.24, f32[2,128,1,16,192]{4,3,0,1,2:T(8,128)S(1)} %fusion.39, ...), kind=kLoop, calls=%fused_computation.64 | loop fusion | flops 13107200 | bytes 12451840 | tf_op jit(solution)/shard_map/sub | solution.py:174
  246.6 1.9 copy.258
  248.5 35.5 %all_to_all.49 = f32[2,128,1,2048]{1,0,2,3:T(2,128)S(1)} all-to-all(f32[2,128,1,2048]{1,0,2,3:T(2,128)} %bitcast.604), channel_id=1, replica_groups=mesh['depth'=8,'lat'=16] {'lat'}, dimensions={3} | all-to-all | bytes 4194304 | tf_op jit(solution)/shard_map/all_to_all | solution.py:176
  284.0 1.6 fusion.265
  285.6 1.4 copy.250
  287.0 1.4 copy.249
  (62 shorter events, 1.2 us)
Async XLA Ops:
  0.6 15.2 %copy-start = (f32[8,4]{0,1:T(4,128)S(1)}, f32[8,4]{0,1:T(4,128)}, u32[]{:S(2)}) copy-start(f32[8,4]{0,1:T(4,128)} %param.11) | copy-start | bytes 388
  7.0 8.1 %copy-start.6 = (f32[3,16,128]{2,1,0:T(8,128)S(1)}, f32[3,16,128]{2,1,0:T(8,128)}, u32[]{:S(2)}) copy-start(f32[3,16,128]{2,1,0:T(8,128)} %param.8) | copy-start | bytes 73732
  7.0 8.8 %copy-start.7 = (s32[3,128]{1,0:T(4,128)S(1)}, s32[3,128]{1,0:T(4,128)}, u32[]{:S(2)}) copy-start(s32[3,128]{1,0:T(4,128)} %param.9) | copy-start | bytes 4612
  7.0 8.8 %copy-start.8 = (s32[3,128]{1,0:T(4,128)S(1)}, s32[3,128]{1,0:T(4,128)}, u32[]{:S(2)}) copy-start(s32[3,128]{1,0:T(4,128)} %param.10) | copy-start | bytes 4612
  7.0 39.9 %all-to-all-start = ((f32[2,128,16,128]{3,0,1,2:T(2,128)}), f32[2,128,16,128]{3,0,1,2:T(2,128)S(1)}, u32[]{:S(2)}, u32[]{:S(2)}) async-start(f32[2,128,16,128]{3,0,1,2:T(2,128)} %pad_maximum_fusion), calls=%async_computation | async-start | bytes 4194304 | tf_op jit(solution)/shard_map/all_to_all | solution.py:130
  46.9 5.7 %copy-start.2 = (f32[2,128,16,128]{3,0,1,2:T(2,128)}, f32[2,128,16,128]{3,0,1,2:T(2,128)S(1)}, u32[]{:S(2)}) copy-start(f32[2,128,16,128]{3,0,1,2:T(2,128)S(1)} %all-to-all-done) | copy-start | bytes 6291460
  46.9 24.8 %all-to-all-start.2 = ((f32[1,3,16,128]{3,0,1,2:T(1,128)}), f32[1,3,16,128]{3,0,1,2:T(1,128)S(1)}, u32[]{:S(2)}, u32[]{:S(2)}) async-start(f32[1,3,16,128]{3,0,1,2:T(1,128)} %copy.206), calls=%async_computation.2 | async-start | bytes 49152 | tf_op jit(solution)/shard_map/all_to_all | solution.py:131
  72.4 10.6 %all-to-all-start.1 = ((f32[8,32,128]{2,1,0:T(8,128)}), f32[8,32,128]{2,1,0:T(8,128)S(1)}, u32[]{:S(2)}, u32[]{:S(2)}) async-start(f32[8,32,128]{2,1,0:T(8,128)} %broadcast_in_dim.227), calls=%async_computation.1 | async-start | bytes 262144 | tf_op jit(solution)/shard_map/all_to_all | solution.py:19
  112.6 1.6 copy-start.3
  138.2 9.4 %all-to-all-start.3 = ((f32[8,32,128]{2,1,0:T(8,128)}), f32[8,32,128]{2,1,0:T(8,128)S(1)}, u32[]{:S(2)}, u32[]{:S(2)}) async-start(f32[8,32,128]{2,1,0:T(8,128)} %broadcast_in_dim.239), calls=%async_computation.3 | async-start | bytes 262144 | tf_op jit(solution)/shard_map/all_to_all | solution.py:19
  177.3 1.6 copy-start.4
  177.4 2.2 copy-start.5
  284.0 4.4 %copy-start.1 = (f32[8,4]{0,1:T(4,128)S(1)}, f32[8,4]{0,1:T(4,128)}, u32[]{:S(2)}) copy-start(f32[8,4]{0,1:T(4,128)} %param.11) | copy-start | bytes 388
where the time goes:
time: 292 us; the launch traced here: 289 us
  matrix products  134 us (46%)
  blocking collectives  44.2 us (15%)
  waiting for transfers between devices  42.4 us (15%)
  other arithmetic  27.7 us (9%)
  local copies, waits for them, and re-layouts  19.7 us (7%)
  starting transfers between devices  19.6 us (7%)
    dot_general x3, matrix products, body(): jnp.einsum('czrtx,zjx->czrtj', jnp.stack([grad_color, grad_density]), ban...  80 us
    dot_general x3, matrix products, body(): jnp.einsum('czrtj,zjx->czrtx', with_margins(fields), banded, precision=HI...  52.9 us
    all_to_all x1, blocking collectives, body(): lax.all_to_all(fields, 'lat', split_axis=3, concat_axis=2, tiled=True)  35.5 us
    all_to_all x1, waiting for transfers between devices, body(): lax.all_to_all(fields, 'lat', split_axis=2, concat_axis=3, tiled=True)  30.3 us
    sub x3, other arithmetic, body(): fields - LEARN_RATE * scaled_first / (jnp.sqrt(scaled_second) + ADAM_EPSI...  12.4 us
    all_to_all x2, waiting for transfers between devices, copy_for_each(): lax.all_to_all(jnp.broadcast_to(x[None], (devices, *x.shape)), axis, 0, 0...  12.1 us
    all_to_all x1, blocking collectives, copy_for_each(): lax.all_to_all(jnp.broadcast_to(x[None], (devices, *x.shape)), axis, 0, 0...  8.7 us
    all_to_all x1, starting transfers between devices, body(): lax.all_to_all(fields, 'lat', split_axis=2, concat_axis=3, tiled=True)  8.12 us
  transfers between devices with their start and end apart: 4, of which 3 were waited for; matrix products, arithmetic and copies ran while one was open for 8% of the time, Pallas kernels for 0%

commit v1 on v0

v1 whole, which is shorter than its diff:
```python
import functools

import jax
import jax.numpy as jnp
from jax import lax
from jax.experimental import pallas as pl
from jax.experimental.pallas import tpu as pltpu
from jax.sharding import PartitionSpec as P

ITERS = 3
LEARN_RATE = 0.1
BETA_FIRST = 0.9
BETA_SECOND = 0.999
ADAM_EPSILON = 0.001

LANES = 128
HALF = 8
TOP = 8
PADDED = 32
GROUP = 8
INTERPRET = False


def halves(ref, *lead):
    return [ref[(*lead, pl.ds(HALF * h, HALF), slice(None))] for h in range(2)]


def put_halves(ref, lead, values):
    for h in range(2):
        ref[(*lead, pl.ds(HALF * h, HALF), slice(None))] = values[h]


def resampled(buf, lead, start, step, weights, lane):
    rows = {
        d: [buf[(*lead, pl.ds(TOP + HALF * h + d, HALF), slice(None))] for h in range(2)]
        for d in (-1, 0, 1)
    }
    total = [None, None]
    for k, weight in enumerate(weights):
        lag = start + step * k
        low = lane < lag
        high = lane >= lag + LANES
        turn = (LANES - lag) & (LANES - 1)
        for h in range(2):
            picked = jnp.where(low, rows[1][h], jnp.where(high, rows[-1][h], rows[0][h]))
            term = weight * pltpu.roll(picked, turn, 1)
            total[h] = term if total[h] is None else total[h] + term
    return total


def plane_weights(fraction_ref, table_ref, view, z):
    row = fraction_ref[view, z]
    return [table_ref[row, k] for k in range(table_ref.shape[1])]


def adam_change(view, grad, first):
    power = view + 1
    if view == 0:
        return LEARN_RATE * grad / (jnp.abs(grad) + ADAM_EPSILON)
    top = grad
    square = grad * grad
    for age, old in enumerate(first):
        top = top + BETA_FIRST ** (age + 1) * old
        square = square + BETA_SECOND ** (age + 1) * (old * old)
    top = top * (LEARN_RATE * (1.0 - BETA_FIRST) / (1.0 - BETA_FIRST**power))
    square = square * ((1.0 - BETA_SECOND) / (1.0 - BETA_SECOND**power))
    return top / (jnp.sqrt(square) + ADAM_EPSILON)


def march(color, density, carry, planes):
    depth, passing, light = carry
    fade = jnp.exp(-jnp.abs(density))
    optical = (jnp.maximum(density, 0.0) + jnp.log1p(fade)) * (1.0 / planes)
    inverse = 1.0 / (1.0 + fade)
    slope = jnp.where(density >= 0.0, inverse, fade * inverse)
    small = optical * (1.0 - optical * (0.5 - optical * (1.0 / 6.0 - optical * (1.0 / 24.0))))
    opacity = jnp.where(optical < 0.03, small, 1.0 - jnp.exp(-optical))
    blend = passing * opacity
    depth = depth + optical
    passing = jnp.exp(-depth)
    light = light + blend * color
    reach = slope * (passing * color + light)
    return (depth, passing, light), (blend, reach, slope)


def clear_edges(buf):
    blank = jnp.zeros((HALF, LANES), jnp.float32)
    for p in range(buf.shape[0]):
        for f in range(buf.shape[1]):
            buf[p, f, pl.ds(0, TOP), :] = blank
            buf[p, f, pl.ds(TOP + 2 * HALF, HALF), :] = blank


def lane_index():
    return lax.broadcasted_iota(jnp.int32, (HALF, LANES), 1)


def fresh_carry():
    zero = jnp.zeros((HALF, LANES), jnp.float32)
    return [(zero, zero + 1.0, zero) for _ in range(2)]


def forward_group(view, base, buf, carry, scalars, outs, lane, planes):
    shift_ref, fraction_ref, table_ref = scalars
    for p in range(GROUP):
        z = base + p
        weights = plane_weights(fraction_ref, table_ref, view, z)
        start = shift_ref[view, z] - 1
        color = resampled(buf, (p, 0), start, 1, weights, lane)
        density = resampled(buf, (p, 1), start, 1, weights, lane)
        for h in range(2):
            carry[h], kept = march(color[h], density[h], carry[h], planes)
            for ref, value in zip(outs, kept):
                ref[z, pl.ds(HALF * h, HALF), :] = value
    return carry


def put_slab(slab_ref, carry):
    put_halves(slab_ref, (0,), [carry[h][2] for h in range(2)])
    put_halves(slab_ref, (1,), [carry[h][0] for h in range(2)])


def first_kernel(planes, shift_ref, fraction_ref, table_ref, sent_ref, e_ref, a_ref, goal_ref,
                 blend_ref, reach_ref, slope_ref, slab_ref, buf, sems):
    depth_planes = e_ref.shape[0]
    tiles = e_ref.shape[1]
    copies = []
    for t in range(tiles):
        for f, ref in enumerate((e_ref, a_ref)):
            copies.append(pltpu.make_async_copy(
                sent_ref.at[t, pl.ds(f * depth_planes, depth_planes), :], ref.at[:, t, :], sems.at[f, t]))
        copies.append(pltpu.make_async_copy(
            sent_ref.at[t, pl.ds(2 * depth_planes, ITERS), :], goal_ref.at[:, t, :], sems.at[2, t]))
    for c in copies:
        c.start()
    clear_edges(buf)
    lane = lane_index()
    for c in copies:
        c.wait()

    def step(i, carry):
        base = i * GROUP
        for p in range(GROUP):
            for f, ref in enumerate((e_ref, a_ref)):
                for h in range(2):
                    buf[p, f, pl.ds(TOP + HALF * h, HALF), :] = ref[base + p, pl.ds(HALF * h, HALF), :]
        return forward_group(0, base, buf, list(carry), (shift_ref, fraction_ref, table_ref),
                             (blend_ref, reach_ref, slope_ref), lane, planes)

    put_slab(slab_ref, lax.fori_loop(0, depth_planes // GROUP, step, fresh_carry()))


def combined_rays(view, here_ref, slabs_ref, goal_ref, planes):
    here = here_ref[0]
    found = []
    for h in range(2):
        rows = pl.ds(HALF * h, HALF)
        depth = jnp.zeros((HALF, LANES), jnp.float32)
        image = depth
        front = depth
        clear = depth + 1.0
        passing = clear
        for i in range(slabs_ref.shape[0]):
            front = jnp.where(here == i, image, front)
            clear = jnp.where(here == i, passing, clear)
            image = image + passing * slabs_ref[i, 0, rows, :]
            depth = depth + slabs_ref[i, 1, rows, :]
            passing = jnp.exp(-depth)
        residual = image - goal_ref[view, rows, :]
        found.append((residual * clear, residual * (image - front)))
    return found


def later_kernel(view, planes, *refs):
    last = view == ITERS - 1
    here_ref, shift_ref, fraction_ref, table_ref, slabs_ref, goal_ref = refs[:6]
    at = 6
    fields = refs[at : at + 2]
    at += 2
    old = [refs[at + 2 * n : at + 2 * n + 2] for n in range(view)][::-1]
    at += 2 * view
    kept = refs[at : at + 3]
    at += 3
    new_fields = refs[at : at + 2]
    at += 2
    if last:
        sent_ref = new_fields[0]
        at -= 1
    else:
        grads = refs[at : at + 2]
        new_kept = refs[at + 2 : at + 5]
        slab_ref = refs[at + 5]
        at += 6
    if last:
        gbuf, store_e, store_a, sems = refs[at:]
        new_fields = (store_e, store_a)
    else:
        gbuf, fbuf = refs[at:]
        clear_edges(fbuf)
    clear_edges(gbuf)
    lane = lane_index()
    rays = combined_rays(view, here_ref, slabs_ref, goal_ref, planes)
    depth_planes = fields[0].shape[0]

    def step(i, carry):
        base = i * GROUP
        for p in range(GROUP):
            for h in range(2):
                rows = pl.ds(HALF * h, HALF)
                blend, reach, slope = (ref[base + p, rows, :] for ref in kept)
                near, far = rays[h]
                gbuf[p, 0, pl.ds(TOP + HALF * h, HALF), :] = (near * planes) * blend
                gbuf[p, 1, pl.ds(TOP + HALF * h, HALF), :] = near * reach - far * slope
        for p in range(GROUP):
            z = base + p
            weights = plane_weights(fraction_ref, table_ref, view, z)
            start = 1 - shift_ref[view, z]
            for f in range(2):
                grad = resampled(gbuf, (p, f), start, -1, weights, lane)
                for h in range(2):
                    rows = pl.ds(HALF * h, HALF)
                    first = [pair[f][z, rows, :] for pair in old]
                    value = fields[f][z, rows, :] - adam_change(view, grad[h], first)
                    new_fields[f][z, rows, :] = value
                    if not last:
                        grads[f][z, rows, :] = grad[h]
                        fbuf[p, f, pl.ds(TOP + HALF * h, HALF), :] = value
        if last:
            return carry
        return forward_group(view + 1, base, fbuf, list(carry), (shift_ref, fraction_ref, table_ref),
                             new_kept, lane, planes)

    if last:
        lax.fori_loop(0, depth_planes // GROUP, step, 0)
        copies = [
            pltpu.make_async_copy(
                ref.at[:, t, :], sent_ref.at[t, pl.ds(f * depth_planes, depth_planes), :], sems.at[f, t])
            for t in range(sent_ref.shape[0])
            for f, ref in enumerate(new_fields)
        ]
        for c in copies:
            c.start()
        for c in copies:
            c.wait()
    else:
        put_slab(slab_ref, lax.fori_loop(0, depth_planes // GROUP, step, fresh_carry()))


def pack_kernel(e_ref, a_ref, goal_ref, sent_ref, sems):
    depth_planes = e_ref.shape[0]
    copies = []
    for t in range(e_ref.shape[1]):
        for f, ref in enumerate((e_ref, a_ref)):
            copies.append(pltpu.make_async_copy(
                ref.at[:, t, :], sent_ref.at[t, pl.ds(f * depth_planes, depth_planes), :], sems.at[f, t]))
        copies.append(pltpu.make_async_copy(
            goal_ref.at[:, t, :], sent_ref.at[t, pl.ds(2 * depth_planes, ITERS), :], sems.at[2, t]))
    for c in copies:
        c.start()
    for c in copies:
        c.wait()


def unpack_kernel(sent_ref, e_ref, a_ref, sems):
    depth_planes = e_ref.shape[0]
    copies = [
        pltpu.make_async_copy(
            sent_ref.at[t, pl.ds(f * depth_planes, depth_planes), :], ref.at[:, t, :], sems.at[f, t])
        for t in range(e_ref.shape[1])
        for f, ref in enumerate((e_ref, a_ref))
    ]
    for c in copies:
        c.start()
    for c in copies:
        c.wait()


ANY = pl.BlockSpec(memory_space=pl.ANY)
VMEM = pl.BlockSpec(memory_space=pltpu.VMEM)
SMEM = pl.BlockSpec(memory_space=pltpu.SMEM)


def call(kernel, in_specs, out_specs, out_shape, scratch, name):
    return pl.pallas_call(
        kernel,
        in_specs=in_specs,
        out_specs=out_specs,
        out_shape=out_shape,
        scratch_shapes=scratch,
        interpret=INTERPRET,
        name=name,
        compiler_params=pltpu.CompilerParams(vmem_limit_bytes=40 * 1024 * 1024),
    )


def body(emission, absorption, target, shift_whole, shift_fraction, taps_table):
    depth_planes, tiles, width = emission.shape
    slabs = lax.axis_size("depth")
    planes = depth_planes * slabs
    here = lax.axis_index("depth").astype(jnp.int32).reshape(1)
    scalars = (shift_whole, shift_fraction, taps_table)
    volume = jax.ShapeDtypeStruct(emission.shape, jnp.float32)
    slab = jax.ShapeDtypeStruct((2, tiles, width), jnp.float32)
    goals = jax.ShapeDtypeStruct((ITERS, tiles, width), jnp.float32)
    padded = pltpu.VMEM((GROUP, 2, PADDED, width), jnp.float32)

    def sems(n):
        return pltpu.SemaphoreType.DMA((n, tiles))

    packed_rows = 2 * depth_planes + 8
    packed = call(
        pack_kernel, [ANY] * 3, ANY, jax.ShapeDtypeStruct((tiles, packed_rows, width), jnp.float32),
        [sems(3)], "pack",
    )(emission, absorption, target)
    packed = lax.all_to_all(packed, "lat", 0, 0, tiled=True)
    e, a, goal, *kept, sums = call(
        functools.partial(first_kernel, planes),
        [SMEM] * 3 + [ANY], [VMEM] * 7,
        [volume, volume, goals, volume, volume, volume, slab],
        [padded, sems(3)], "first",
    )(*scalars, packed)
    old = []
    for view in range(ITERS):
        everyone = lax.all_to_all(
            jnp.broadcast_to(sums[None], (slabs, *sums.shape)), "depth", 0, 0, tiled=True)
        last = view == ITERS - 1
        operands = (here, *scalars, everyone, goal, e, a, *old, *kept)
        in_specs = [SMEM] * 4 + [VMEM] * (len(operands) - 4)
        kernel = functools.partial(later_kernel, view, planes)
        if last:
            packed = call(
                kernel, in_specs, ANY, jax.ShapeDtypeStruct((tiles, 2 * depth_planes, width), jnp.float32),
                [padded, pltpu.VMEM(emission.shape, jnp.float32), pltpu.VMEM(emission.shape, jnp.float32), sems(2)],
                "last",
            )(*operands)
        else:
            e, a, g_e, g_a, *kept, sums = call(
                kernel, in_specs, [VMEM] * 8, [volume] * 7 + [slab], [padded, padded], "middle",
            )(*operands)
            old = [*old, g_e, g_a]
    packed = lax.all_to_all(packed, "lat", 0, 0, tiled=True)
    return call(unpack_kernel, [ANY], [ANY, ANY], [volume, volume], [sems(2)], "unpack")(packed)


def solution(mesh):
    in_specs = (
        P("depth", None, "lat"),
        P("depth", None, "lat"),
        P(None, None, "lat"),
        P(None, "depth"),
        P(None, "depth"),
        P(),
    )
    out_specs = (P("depth", None, "lat"), P("depth", None, "lat"))
    return jax.shard_map(body, mesh=mesh, in_specs=in_specs, out_specs=out_specs, check_vma=False)
```

time: 292 us -> 148 us (0.51)
  matrix products: 134 us -> 0 us
  Pallas kernels: 0 us -> 31.9 us
  other arithmetic: 27.7 us -> 0 us
  starting transfers between devices: 19.6 us -> 12.6 us
  local copies, waits for them, and re-layouts: 19.7 us -> 15.1 us
  blocking collectives: 44.2 us -> 48.6 us
  waiting for transfers between devices: 42.4 us -> 38.7 us
    dot_general x9 -> x0, matrix products: 134 us -> none  [the longest x3 80 us: body(): jnp.einsum('czrtx,zjx->czrtj', jnp.stack([grad_color, grad_density]), ban...]
    pallas_call x0 -> x6, Pallas kernels: none -> 31.9 us  [the longest x2 15 us: body(): call(kernel, in_specs, [VMEM] * 8, [volume] * 7 + [slab], [padded, padded...]
    sub x4 -> x0, other arithmetic: 12.4 us -> none  [the longest x3 12.4 us: body(): fields - LEARN_RATE * scaled_first / (jnp.sqrt(scaled_second) + ADAM_EPSI...]
    another operation x7 -> x0, other arithmetic: 11.3 us -> none  [the longest x3 4.61 us: body(): behind = rendered - front_light - attenuate * jnp.cumsum(emitted, axis=0)]
    all_to_all x4 -> x2, starting transfers between devices: 19.6 us -> 12.6 us  [the longest x1 8.12 us: body(): packed = lax.all_to_all(packed, 'lat', 0, 0, tiled=True)]
    slice x14 -> x0, local copies, waits for them, and re-layouts: 6.53 us -> none  [the longest x3 2.5 us: fold_margins(): from_left = jnp.concatenate([blank, right_rim[:, :, :, :-1]], axis=3)]
    unnamed x22 -> x33, local copies, waits for them, and re-layouts: 8.02 us -> 14.4 us
    all_to_all x2 -> x3, blocking collectives: 44.2 us -> 48.6 us  [the longest x1 31.6 us: body(): packed = lax.all_to_all(packed, 'lat', 0, 0, tiled=True)]
  transfers between devices with their start and end apart: 4 -> 2, of which waited for: 3 -> 2; matrix products, arithmetic and copies ran while one was open for 8% -> 0% of each run, Pallas kernels for 0% -> 0%
where the time goes in v1:
time: 148 us
  blocking collectives  48.6 us (33%)
  waiting for transfers between devices  38.7 us (26%)
  Pallas kernels  31.9 us (22%)
  local copies, waits for them, and re-layouts  15.1 us (10%)
  starting transfers between devices  12.6 us (9%)
    all_to_all x1, waiting for transfers between devices, body(): packed = lax.all_to_all(packed, 'lat', 0, 0, tiled=True)  32.6 us
    all_to_all x1, blocking collectives, body(): packed = lax.all_to_all(packed, 'lat', 0, 0, tiled=True)  31.6 us
    all_to_all x2, blocking collectives, body(): lax.all_to_all(jnp.broadcast_to(sums[None], (slabs, *sums.shape)), 'depth...  17 us
    pallas_call x2, Pallas kernels, body(): call(kernel, in_specs, [VMEM] * 8, [volume] * 7 + [slab], [padded, padded...  15 us
    unnamed x33, local copies, waits for them, and re-layouts  14.4 us
    all_to_all x1, starting transfers between devices, body(): packed = lax.all_to_all(packed, 'lat', 0, 0, tiled=True)  8.12 us
    pallas_call x1, Pallas kernels, body(): call(kernel, in_specs, ANY, jax.ShapeDtypeStruct((tiles, 2 * depth_planes...  6.79 us
    pallas_call x1, Pallas kernels, body(): call(functools.partial(first_kernel, planes), [SMEM] * 3 + [ANY], [VMEM]...  6.54 us
  transfers between devices with their start and end apart: 2, of which 2 were waited for; matrix products, arithmetic and copies ran while one was open for 0% of the time, Pallas kernels for 0%

profile of v1, /device:TPU:0, one launch (start us, length us, event | category | flops | bytes accessed | tf_op | source)
XLA Modules:
  0.0 147.6 jit_solution(13098146369395741370)
XLA Ops:
  0.6 0.0 copy-start.1
  0.6 1.2 copy-done.1
  1.9 0.0 copy-start.2
  1.9 1.2 copy-done.2
  3.1 0.0 copy-start.14
  3.1 0.7 copy-done.14
  3.8 2.0 %pack.1 = f32[16,264,128]{2,1,0:T(8,128)S(1)} custom-call(f32[128,16,128]{2,1,0:T(8,128)S(1)} %copy-done.1, f32[128,16,128]{2,1,0:T(8,128)S(1)} %copy-done.2, f32[3,16,128]{2,1,0:T(8,128)S(1)} %copy-done.14), custom_call_target="tpu_custom_call" | custom-call | tf_op jit(solution)/shard_map/pack/pallas_call | solution.py:311
  5.8 0.0 copy-start
  5.8 1.3 copy-done
  7.2 0.0 copy-start.15
  7.2 0.0 copy-start.12
  7.2 0.0 copy-start.13
  7.2 8.1 %all-to-all-start = ((f32[16,264,128]{2,1,0:T(8,128)}), f32[16,264,128]{2,1,0:T(8,128)S(1)}, u32[]{:S(2)}, u32[]{:S(2)}) async-start(f32[16,264,128]{2,1,0:T(8,128)} %copy-done), calls=%async_computation | async-start | bytes 4325376 | tf_op jit(solution)/shard_map/all_to_all | solution.py:315
  15.3 0.0 copy-done.15
  15.3 0.1 copy.11.table_ref.refs_3_
  15.4 32.6 %all-to-all-done.sent_ref = f32[16,264,128]{2,1,0:T(8,128)S(1)} async-done(((f32[16,264,128]{2,1,0:T(8,128)}), f32[16,264,128]{2,1,0:T(8,128)S(1)}, u32[]{:S(2)}, u32[]{:S(2)}) %all-to-all-start) | async-done | bytes 2162720 | tf_op jit(solution)/shard_map/all_to_all | solution.py:315
  48.0 0.0 copy-done.12
  48.0 0.0 copy-done.13
  48.0 6.5 %first.1 = (f32[128,16,128]{2,1,0:T(8,128)S(1)}, f32[128,16,128]{2,1,0:T(8,128)S(1)}, f32[3,16,128]{2,1,0:T(8,128)S(1)}, f32[128,16,128]{2,1,0:T(8,128)S(1)}, f3...) custom-call(s32[3,128]{1,0:T(4,128)S(1)} %copy-done.12, ...), custom_call_target="tpu_custom_call" | custom-call | tf_op jit(solution)/shard_map/first/pallas_call | solution.py:316
  54.6 0.0 copy-start.3
  54.6 1.0 copy-done.3
  55.5 0.0 copy-start.5
  55.6 1.0 copy-done.5
  56.5 0.0 copy-start.7
  56.5 1.0 copy-done.7
  57.5 0.0 copy-start.9
  57.5 1.0 copy-done.9
  58.5 0.7 broadcast_in_dim.6
  59.2 4.5 %all-to-all-start.1 = ((f32[8,2,16,128]{3,2,1,0:T(8,128)}), f32[8,2,16,128]{3,2,1,0:T(8,128)S(1)}, u32[]{:S(2)}, u32[]{:S(2)}) async-start(f32[8,2,16,128]{3,2,1,0:T(8,128)} %broadcast_in_dim.6), calls=%async_computation.1 | async-start | bytes 262144 | tf_op jit(solution)/shard_map/all_to_all | solution.py:324
  63.6 6.1 %all-to-all-done.1.refs_4_ = f32[8,2,16,128]{3,2,1,0:T(8,128)S(1)} async-done(((f32[8,2,16,128]{3,2,1,0:T(8,128)}), f32[8,2,16,128]{3,2,1,0:T(8,128)S(1)}, u32[]{:S(2)}, u32[]{:S(2)}) %all-to-all-start.1) | async-done | bytes 131104 | tf_op jit(solution)/shard_map/all_to_all | solution.py:324
  69.7 0.0 copy-start.4
  69.7 1.2 copy-done.4
  71.0 0.0 copy-start.6
  71.0 1.2 copy-done.6
  72.2 0.0 copy-start.8
  72.2 1.2 copy-done.8
  73.4 0.0 copy-start.10
  73.4 1.2 copy-done.10
  74.6 6.9 %middle.2 = (f32[128,16,128]{2,1,0:T(8,128)S(1)}, f32[128,16,128]{2,1,0:T(8,128)S(1)}, f32[128,16,128]{2,1,0:T(8,128)S(1)}, f32[128,16,128]{2,1,0:T(8,128)S(1)},...) custom-call(s32[1]{0:T(128)} %bitcast.refs_0_, ...), custom_call_target="tpu_custom_call" | custom-call | tf_op jit(solution)/shard_map/middle/pallas_call | solution.py:337
  81.6 0.0 copy-start.11
  81.6 1.0 copy-done.11
  82.6 8.5 %all_to_all.25.refs_4_ = f32[8,2,16,128]{3,2,1,0:T(8,128)S(1)} all-to-all(f32[8,2,16,128]{3,2,1,0:T(8,128)S(1)} %broadcast_in_dim.7), channel_id=1, replica_groups=mesh['depth'=8,'lat'=16] {'depth'}, dimensions={0} | all-to-all | bytes 262144 | tf_op jit(solution)/shard_map/all_to_all | solution.py:324
  91.0 8.1 %middle.3 = (f32[128,16,128]{2,1,0:T(8,128)S(1)}, f32[128,16,128]{2,1,0:T(8,128)S(1)}, f32[128,16,128]{2,1,0:T(8,128)S(1)}, f32[128,16,128]{2,1,0:T(8,128)S(1)},...) custom-call(s32[1]{0:T(128)} %bitcast.refs_0_, ...), custom_call_target="tpu_custom_call" | custom-call | tf_op jit(solution)/shard_map/middle/pallas_call | solution.py:337
  99.2 8.5 %all_to_all.26.refs_4_ = f32[8,2,16,128]{3,2,1,0:T(8,128)S(1)} all-to-all(f32[8,2,16,128]{3,2,1,0:T(8,128)S(1)} %broadcast_in_dim.8), channel_id=1, replica_groups=mesh['depth'=8,'lat'=16] {'depth'}, dimensions={0} | all-to-all | bytes 262144 | tf_op jit(solution)/shard_map/all_to_all | solution.py:324
  107.6 6.8 %last.1 = f32[16,256,128]{2,1,0:T(8,128)S(1)} custom-call(s32[1]{0:T(128)} %bitcast.refs_0_, s32[3,128]{1,0:T(4,128)S(1)} %copy-done.12, s32[3,128]{1,0:T(4,128)S(1)} %copy-done.13, f32[8,4]{1,0:T(8,128)S(1)} %copy.11.table_ref.refs_3_, f32[8,2,16,128]{3,2,1,0:T(8,128)S(1)} %all_to_all.26.refs_4_, f32[3,16,128]{2,1,0:T(8,128)S(1)} %get-tuple-element.26.refs_5_, ...), custom_call_target="tpu_custom_call" | custom-call | tf_op jit(solution)/shard_map/last/pallas_call | solution.py:331
  114.4 31.6 %all_to_all.27.sent_ref = f32[16,256,128]{2,1,0:T(8,128)S(1)} all-to-all(f32[16,256,128]{2,1,0:T(8,128)S(1)} %last.1), channel_id=1, replica_groups=mesh['depth'=8,'lat'=16] {'lat'}, dimensions={0} | all-to-all | bytes 4194304 | tf_op jit(solution)/shard_map/all_to_all | solution.py:341
  146.0 1.6 %unpack.1 = (f32[128,16,128]{2,1,0:T(8,128)}, f32[128,16,128]{2,1,0:T(8,128)}) custom-call(f32[16,256,128]{2,1,0:T(8,128)S(1)} %all_to_all.27.sent_ref), custom_call_target="tpu_custom_call" | custom-call | tf_op jit(solution)/shard_map/unpack/pallas_call | solution.py:342
  (2 shorter events, 0.0 us)
Async XLA Ops:
  0.6 1.2 copy-start.1
  1.9 1.2 copy-start.2
  3.1 0.7 copy-start.14
  5.8 1.3 copy-start
  7.2 8.1 %copy-start.15 = (f32[8,4]{0,1:T(4,128)S(1)}, f32[8,4]{0,1:T(4,128)}, u32[]{:S(2)}) copy-start(f32[8,4]{0,1:T(4,128)} %param.11) | copy-start | bytes 388
  7.2 40.9 %copy-start.12 = (s32[3,128]{1,0:T(4,128)S(1)}, s32[3,128]{1,0:T(4,128)}, u32[]{:S(2)}) copy-start(s32[3,128]{1,0:T(4,128)} %refs_1_.5) | copy-start | bytes 4612
  7.2 40.9 %copy-start.13 = (s32[3,128]{1,0:T(4,128)S(1)}, s32[3,128]{1,0:T(4,128)}, u32[]{:S(2)}) copy-start(s32[3,128]{1,0:T(4,128)} %refs_2_.5) | copy-start | bytes 4612
  7.2 40.9 %all-to-all-start = ((f32[16,264,128]{2,1,0:T(8,128)}), f32[16,264,128]{2,1,0:T(8,128)S(1)}, u32[]{:S(2)}, u32[]{:S(2)}) async-start(f32[16,264,128]{2,1,0:T(8,128)} %copy-done), calls=%async_computation | async-start | bytes 4325376 | tf_op jit(solution)/shard_map/all_to_all | solution.py:315
  54.6 1.0 copy-start.3
  55.5 1.0 copy-start.5
  56.5 1.0 copy-start.7
  57.5 1.0 copy-start.9
  59.2 10.6 %all-to-all-start.1 = ((f32[8,2,16,128]{3,2,1,0:T(8,128)}), f32[8,2,16,128]{3,2,1,0:T(8,128)S(1)}, u32[]{:S(2)}, u32[]{:S(2)}) async-start(f32[8,2,16,128]{3,2,1,0:T(8,128)} %broadcast_in_dim.6), calls=%async_computation.1 | async-start | bytes 262144 | tf_op jit(solution)/shard_map/all_to_all | solution.py:324
  69.7 1.2 copy-start.4
  71.0 1.2 copy-start.6
  72.2 1.2 copy-start.8
  73.4 1.2 copy-start.10
  81.6 1.0 copy-start.11

commit v2 on v1

v2 whole, which is shorter than its diff:
```python
import functools

import jax
import jax.numpy as jnp
from jax import lax
from jax.experimental import pallas as pl
from jax.experimental.pallas import tpu as pltpu
from jax.sharding import PartitionSpec as P

ITERS = 3
LEARN_RATE = 0.1
BETA_FIRST = 0.9
BETA_SECOND = 0.999
ADAM_EPSILON = 0.001
LOG2E = 1.4426950408889634

LANES = 128
HALF = 8
TOP = 8
PADDED = 32
GROUP = 16
CHUNKS = 4
INTERPRET = False


def halves(ref, *lead):
    return [ref[(*lead, pl.ds(HALF * h, HALF), slice(None))] for h in range(2)]


def put_halves(ref, lead, values):
    for h in range(2):
        ref[(*lead, pl.ds(HALF * h, HALF), slice(None))] = values[h]


def resampled(buf, lead, start, step, weights, lane):
    total = [None, None]
    for k, weight in enumerate(weights):
        lag = start + step * k
        behind = lag >> 31
        wrapped = lane < (lag & (LANES - 1))
        turn = (-lag) & (LANES - 1)
        for h in range(2):
            here = buf[(*lead, pl.ds(behind + (TOP + HALF * h), HALF), slice(None))]
            after = buf[(*lead, pl.ds(behind + (TOP + HALF * h + 1), HALF), slice(None))]
            term = weight * pltpu.roll(jnp.where(wrapped, after, here), turn, 1)
            total[h] = term if total[h] is None else total[h] + term
    return total


def plane_weights(fraction_ref, table_ref, view, z):
    column = fraction_ref[view, z]
    return [table_ref[k, column] for k in range(table_ref.shape[0])]


def adam_change(view, grad, first):
    power = view + 1
    if view == 0:
        return LEARN_RATE * grad / (jnp.abs(grad) + ADAM_EPSILON)
    top = grad
    square = grad * grad
    for age, old in enumerate(first):
        top = top + BETA_FIRST ** (age + 1) * old
        square = square + BETA_SECOND ** (age + 1) * (old * old)
    top = top * (LEARN_RATE * (1.0 - BETA_FIRST) / (1.0 - BETA_FIRST**power))
    square = square * ((1.0 - BETA_SECOND) / (1.0 - BETA_SECOND**power))
    return top / (jnp.sqrt(square) + ADAM_EPSILON)


def march(color, density, carry, planes):
    depth, passing, light = carry
    density = density * LOG2E
    fade = jnp.exp2(-jnp.abs(density))
    whole = 1.0 + fade
    soft = jnp.maximum(density, 0.0) + (jnp.log2(whole) + (fade - (whole - 1.0)) * LOG2E)
    slope = jnp.exp2(density - soft)
    optical = soft * (1.0 / (planes * LOG2E))
    series = optical * (1.0 - optical * (0.5 - optical * (1.0 / 6.0)))
    opacity = jnp.where(optical < 0.01, series, 1.0 - jnp.exp2(soft * (-1.0 / planes)))
    blend = passing * opacity
    depth = depth + soft
    passing = jnp.exp2(depth * (-1.0 / planes))
    light = light + blend * color
    reach = slope * (passing * color + light)
    return (depth, passing, light), (blend, reach, slope)


def clear_edges(buf):
    blank = jnp.zeros((HALF, LANES), jnp.float32)
    for p in range(buf.shape[0]):
        for f in range(buf.shape[1]):
            buf[p, f, pl.ds(0, TOP), :] = blank
            buf[p, f, pl.ds(TOP + 2 * HALF, HALF), :] = blank


def lane_index():
    return lax.broadcasted_iota(jnp.int32, (HALF, LANES), 1)


def fresh_carry():
    zero = jnp.zeros((HALF, LANES), jnp.float32)
    return [(zero, zero + 1.0, zero) for _ in range(2)]


def forward_group(view, base, buf, carry, scalars, outs, lane, planes):
    shift_ref, fraction_ref, table_ref = scalars
    for p in range(GROUP):
        z = base + p
        weights = plane_weights(fraction_ref, table_ref, view, z)
        start = shift_ref[view, z] - 1
        color = resampled(buf, (p, 0), start, 1, weights, lane)
        density = resampled(buf, (p, 1), start, 1, weights, lane)
        for h in range(2):
            carry[h], kept = march(color[h], density[h], carry[h], planes)
            for ref, value in zip(outs, kept):
                ref[z, pl.ds(HALF * h, HALF), :] = value
    return carry


def put_slab(slab_ref, carry):
    for i in range(slab_ref.shape[0]):
        put_halves(slab_ref, (i, 0), [carry[h][2] for h in range(2)])
        put_halves(slab_ref, (i, 1), [carry[h][0] for h in range(2)])


def first_kernel(planes, shift_ref, fraction_ref, table_ref, sent_ref, e_ref, a_ref, goal_ref,
                 blend_ref, reach_ref, slope_ref, slab_ref, buf):
    depth_planes = e_ref.shape[0]
    clear_edges(buf)
    lane = lane_index()
    for t in range(goal_ref.shape[1]):
        goal_ref[:, t, :] = sent_ref[t, pl.ds(2 * depth_planes, ITERS), :]

    def step(i, carry):
        base = pl.multiple_of(i * GROUP, GROUP)
        for f, ref in enumerate((e_ref, a_ref)):
            for g in range(GROUP // HALF):
                for h in range(2):
                    rows = pl.ds(HALF * h, HALF)
                    block = jnp.transpose(
                        sent_ref[rows, pl.ds(f * depth_planes + base + g * HALF, HALF), :], (1, 0, 2))
                    ref[pl.ds(base + g * HALF, HALF), rows, :] = block
                    buf[pl.ds(g * HALF, HALF), f, pl.ds(TOP + HALF * h, HALF), :] = block
        return forward_group(0, base, buf, list(carry), (shift_ref, fraction_ref, table_ref),
                             (blend_ref, reach_ref, slope_ref), lane, planes)

    put_slab(slab_ref, lax.fori_loop(0, depth_planes // GROUP, step, fresh_carry()))


def combined_rays(view, slabs_ref, goal_ref, planes):
    here = lax.axis_index("depth")
    found = []
    for h in range(2):
        rows = pl.ds(HALF * h, HALF)
        depth = jnp.zeros((HALF, LANES), jnp.float32)
        image = depth
        front = depth
        clear = depth + 1.0
        passing = clear
        for i in range(slabs_ref.shape[0]):
            front = jnp.where(here == i, image, front)
            clear = jnp.where(here == i, passing, clear)
            image = image + passing * slabs_ref[i, 0, rows, :]
            depth = depth + slabs_ref[i, 1, rows, :]
            passing = jnp.exp2(depth * (-1.0 / planes))
        residual = image - goal_ref[view, rows, :]
        near = residual * clear
        found.append((near * planes, near, residual * (image - front)))
    return found


def later_kernel(view, planes, *refs):
    last = view == ITERS - 1
    refs = list(refs)

    def take(n):
        taken = refs[:n]
        del refs[:n]
        return taken

    shift_ref, fraction_ref, table_ref, slabs_ref, goal_ref = take(5)
    fields = take(2)
    old = [take(2) for _ in range(view)][::-1]
    kept = take(3)
    if last:
        (sent_ref,) = take(1)
        gbuf, fbuf = refs
    else:
        new_fields, grads, new_kept, (slab_ref,) = take(2), take(2), take(3), take(1)
        gbuf, fbuf = refs
        clear_edges(fbuf)
    clear_edges(gbuf)
    lane = lane_index()
    rays = combined_rays(view, slabs_ref, goal_ref, planes)
    depth_planes = fields[0].shape[0]

    def step(i, carry):
        base = pl.multiple_of(i * GROUP, GROUP)
        for p in range(GROUP):
            for h in range(2):
                rows = pl.ds(HALF * h, HALF)
                blend, reach, slope = (ref[base + p, rows, :] for ref in kept)
                scaled, near, far = rays[h]
                gbuf[p, 0, pl.ds(TOP + HALF * h, HALF), :] = scaled * blend
                gbuf[p, 1, pl.ds(TOP + HALF * h, HALF), :] = near * reach - far * slope
        for p in range(GROUP):
            z = base + p
            weights = plane_weights(fraction_ref, table_ref, view, z)
            start = 1 - shift_ref[view, z]
            for f in range(2):
                grad = resampled(gbuf, (p, f), start, -1, weights, lane)
                for h in range(2):
                    rows = pl.ds(HALF * h, HALF)
                    first = [pair[f][z, rows, :] for pair in old]
                    value = fields[f][z, rows, :] - adam_change(view, grad[h], first)
                    fbuf[p, f, pl.ds(TOP + HALF * h, HALF), :] = value
                    if not last:
                        new_fields[f][z, rows, :] = value
                        grads[f][z, rows, :] = grad[h]
        if last:
            for f in range(2):
                for g in range(GROUP // HALF):
                    for h in range(2):
                        block = fbuf[pl.ds(g * HALF, HALF), f, pl.ds(TOP + HALF * h, HALF), :]
                        sent_ref[pl.ds(HALF * h, HALF), pl.ds(f * depth_planes + base + g * HALF, HALF), :] = (
                            jnp.transpose(block, (1, 0, 2)))
            return carry
        return forward_group(view + 1, base, fbuf, list(carry), (shift_ref, fraction_ref, table_ref),
                             new_kept, lane, planes)

    if last:
        lax.fori_loop(0, depth_planes // GROUP, step, 0)
    else:
        put_slab(slab_ref, lax.fori_loop(0, depth_planes // GROUP, step, fresh_carry()))


def pack_kernel(e_ref, a_ref, goal_ref, shift_ref, fraction_ref, table_ref,
                sent_ref, shift_out, fraction_out, table_out,
                e_buf, a_buf, goal_buf, sems, small_sems):
    depth_planes = e_ref.shape[0]
    span = depth_planes // CHUNKS
    copies = [
        [pltpu.make_async_copy(ref.at[pl.ds(c * span, span)], buf.at[pl.ds(c * span, span)], sems.at[f, c])
         for c in range(CHUNKS)]
        for f, (ref, buf) in enumerate(((e_ref, e_buf), (a_ref, a_buf)))
    ]
    small = [
        pltpu.make_async_copy(ref, buf, small_sems.at[n])
        for n, (ref, buf) in enumerate((
            (goal_ref, goal_buf), (shift_ref, shift_out), (fraction_ref, fraction_out), (table_ref, table_out)))
    ]
    for c in [*copies[0], *copies[1], *small]:
        c.start()
    for f, buf in enumerate((e_buf, a_buf)):
        for c in range(CHUNKS):
            copies[f][c].wait()
            for g in range(span // HALF):
                z = c * span + g * HALF
                for h in range(2):
                    rows = pl.ds(HALF * h, HALF)
                    sent_ref[rows, pl.ds(f * depth_planes + z, HALF), :] = jnp.transpose(
                        buf[pl.ds(z, HALF), rows, :], (1, 0, 2))
    for c in small:
        c.wait()
    for t in range(goal_ref.shape[1]):
        sent_ref[t, pl.ds(2 * depth_planes, ITERS), :] = goal_buf[:, t, :]


def unpack_kernel(sent_ref, e_ref, a_ref, e_buf, a_buf, sems):
    depth_planes = e_ref.shape[0]
    span = depth_planes // CHUNKS
    copies = []
    for f, (ref, buf) in enumerate(((e_ref, e_buf), (a_ref, a_buf))):
        for c in range(CHUNKS):
            for g in range(span // HALF):
                z = c * span + g * HALF
                for h in range(2):
                    rows = pl.ds(HALF * h, HALF)
                    buf[pl.ds(z, HALF), rows, :] = jnp.transpose(
                        sent_ref[rows, pl.ds(f * depth_planes + z, HALF), :], (1, 0, 2))
            copy = pltpu.make_async_copy(
                buf.at[pl.ds(c * span, span)], ref.at[pl.ds(c * span, span)], sems.at[f, c])
            copy.start()
            copies.append(copy)
    for copy in copies:
        copy.wait()


HBM = pl.BlockSpec(memory_space=pltpu.HBM)
VMEM = pl.BlockSpec(memory_space=pltpu.VMEM)
SMEM = pl.BlockSpec(memory_space=pltpu.SMEM)


def call(kernel, in_specs, out_specs, out_shape, scratch, name):
    return pl.pallas_call(
        kernel,
        in_specs=in_specs,
        out_specs=out_specs,
        out_shape=out_shape,
        scratch_shapes=scratch,
        interpret=INTERPRET,
        name=name,
        compiler_params=pltpu.CompilerParams(vmem_limit_bytes=16 * 1024 * 1024),
    )


def body(emission, absorption, target, shift_whole, shift_fraction, taps_table):
    depth_planes, tiles, width = emission.shape
    slabs = lax.axis_size("depth")
    planes = depth_planes * slabs
    volume = jax.ShapeDtypeStruct(emission.shape, jnp.float32)
    slab = jax.ShapeDtypeStruct((slabs, 2, tiles, width), jnp.float32)
    goals = jax.ShapeDtypeStruct((ITERS, tiles, width), jnp.float32)
    padded = pltpu.VMEM((GROUP, 2, PADDED, width), jnp.float32)
    store = pltpu.VMEM(emission.shape, jnp.float32)
    sems = pltpu.SemaphoreType.DMA((2, CHUNKS))

    raw = [
        pltpu.with_memory_space_constraint(x, pltpu.HBM)
        for x in (emission, absorption, target, shift_whole, shift_fraction, taps_table.T)
    ]
    packed, *scalars = call(
        pack_kernel, [HBM] * 6, [VMEM] * 4,
        [jax.ShapeDtypeStruct((tiles, 2 * depth_planes + HALF, width), jnp.float32)]
        + [jax.ShapeDtypeStruct(x.shape, x.dtype) for x in raw[3:]],
        [store, store, pltpu.VMEM(target.shape, jnp.float32), sems, pltpu.SemaphoreType.DMA((4,))], "pack",
    )(*raw)
    packed = lax.all_to_all(packed, "lat", 0, 0, tiled=True)
    e, a, goal, *kept, sums = call(
        functools.partial(first_kernel, planes), [SMEM] * 3 + [VMEM], [VMEM] * 7,
        [volume, volume, goals, volume, volume, volume, slab], [padded], "first",
    )(*scalars, packed)
    old = []
    for view in range(ITERS):
        everyone = lax.all_to_all(sums, "depth", 0, 0, tiled=True)
        operands = (*scalars, everyone, goal, e, a, *old, *kept)
        in_specs = [SMEM] * 3 + [VMEM] * (len(operands) - 3)
        kernel = functools.partial(later_kernel, view, planes)
        if view == ITERS - 1:
            packed = call(
                kernel, in_specs, VMEM,
                jax.ShapeDtypeStruct((tiles, 2 * depth_planes, width), jnp.float32), [padded, padded], "last",
            )(*operands)
        else:
            e, a, g_e, g_a, *kept, sums = call(
                kernel, in_specs, [VMEM] * 8, [volume] * 7 + [slab], [padded, padded], "middle",
            )(*operands)
            old = [*old, g_e, g_a]
    packed = lax.all_to_all(packed, "lat", 0, 0, tiled=True)
    return call(
        unpack_kernel, [VMEM], [HBM, HBM], [volume, volume], [store, store, sems], "unpack")(packed)


def solution(mesh):
    in_specs = (
        P("depth", None, "lat"),
        P("depth", None, "lat"),
        P(None, None, "lat"),
        P(None, "depth"),
        P(None, "depth"),
        P(),
    )
    out_specs = (P("depth", None, "lat"), P("depth", None, "lat"))
    return jax.shard_map(body, mesh=mesh, in_specs=in_specs, out_specs=out_specs, check_vma=False)
```

time: 148 us -> 123 us (0.83)
  blocking collectives: 48.6 us -> 95.7 us
  waiting for transfers between devices: 38.7 us -> 0 us
  local copies, waits for them, and re-layouts: 15.1 us -> 0 us
  starting transfers between devices: 12.6 us -> 0 us
  Pallas kernels: 31.9 us -> 26.5 us
    all_to_all x2 -> x0, waiting for transfers between devices: 38.7 us -> none  [the longest x1 32.6 us: body(): packed = lax.all_to_all(packed, 'lat', 0, 0, tiled=True)]
    all_to_all x1 -> x2, blocking collectives: 31.6 us -> 68.2 us  [body(): packed = lax.all_to_all(packed, 'lat', 0, 0, tiled=True)]
    unnamed x33 -> x0, local copies, waits for them, and re-layouts: 14.4 us -> none
    all_to_all x2 -> x0, starting transfers between devices: 12.6 us -> none  [the longest x1 8.12 us: body(): packed = lax.all_to_all(packed, 'lat', 0, 0, tiled=True)]
    all_to_all x2 -> x3, blocking collectives: 17 us -> 27.4 us  [body(): everyone = lax.all_to_all(sums, 'depth', 0, 0, tiled=True)]
    pallas_call x4, Pallas kernels: 16.9 us -> 12.7 us  [the longest x1 5.31 us: body(): call(kernel, in_specs, VMEM, jax.ShapeDtypeStruct((tiles, 2 * depth_plane...]
  transfers between devices with their start and end apart: 2 -> 0, of which waited for: 2 -> 0; matrix products, arithmetic and copies ran while one was open for 0% -> 0% of each run, Pallas kernels for 0% -> 0%
where the time goes in v2:
time: 123 us
  blocking collectives  95.7 us (78%)
  Pallas kernels  26.5 us (22%)
    all_to_all x2, blocking collectives, body(): packed = lax.all_to_all(packed, 'lat', 0, 0, tiled=True)  68.2 us
    all_to_all x3, blocking collectives, body(): everyone = lax.all_to_all(sums, 'depth', 0, 0, tiled=True)  27.4 us
    pallas_call x2, Pallas kernels, body(): call(kernel, in_specs, [VMEM] * 8, [volume] * 7 + [slab], [padded, padded...  13.8 us
    pallas_call x1, Pallas kernels, body(): call(kernel, in_specs, VMEM, jax.ShapeDtypeStruct((tiles, 2 * depth_plane...  5.31 us
    pallas_call x1, Pallas kernels, body(): call(functools.partial(first_kernel, planes), [SMEM] * 3 + [VMEM], [VMEM]...  4.22 us

profile of v2, /device:TPU:0, one launch (start us, length us, event | category | flops | bytes accessed | tf_op | source)
XLA Modules:
  0.0 122.9 jit_solution(14576424973993059613)
XLA Ops:
  0.6 1.7 %pack.1 = (f32[16,264,128]{2,1,0:T(8,128)S(1)}, s32[3,128]{1,0:T(4,128)S(1)}, s32[3,128]{1,0:T(4,128)S(1)}, f32[4,8]{1,0:T(4,128)S(1)}) custom-call(f32[128,16,128]{2,1,0:T(8,128)} %e_ref.1, f32[128,16,128]{2,1,0:T(8,128)} %a_ref.1, f32[3,16,128]{2,1,0:T(8,128)} %goal_ref.1, s32[3,128]{1,0:T(4,128)} %shift_ref.1, s32[3,128]{1,0:T(4,128)} %fraction_ref.1, ...), custom_call_target="tpu_custom_call" | custom-call | tf_op jit(solution)/shard_map/pack/pallas_call | solution.py:321
  2.4 36.9 %all_to_all.25.sent_ref = f32[16,264,128]{2,1,0:T(8,128)S(1)} all-to-all(f32[16,264,128]{2,1,0:T(8,128)S(1)} %get-tuple-element.32), channel_id=1, replica_groups=mesh['depth'=8,'lat'=16] {'lat'}, dimensions={0} | all-to-all | bytes 4325376 | tf_op jit(solution)/shard_map/all_to_all | solution.py:327
  39.3 4.2 %first.1 = (f32[128,16,128]{2,1,0:T(8,128)S(1)}, f32[128,16,128]{2,1,0:T(8,128)S(1)}, f32[3,16,128]{2,1,0:T(8,128)S(1)}, f32[128,16,128]{2,1,0:T(8,128)S(1)}, f3...) custom-call(s32[3,128]{1,0:T(4,128)S(1)} %get-tuple-element.29.shift_ref.refs_0_, ...), custom_call_target="tpu_custom_call" | custom-call | tf_op jit(solution)/shard_map/first/pallas_call | solution.py:328
  43.5 10.4 %all_to_all.26.refs_3_ = f32[8,2,16,128]{3,2,1,0:T(8,128)S(1)} all-to-all(f32[8,2,16,128]{3,2,1,0:T(8,128)S(1)} %get-tuple-element.33), channel_id=1, replica_groups=mesh['depth'=8,'lat'=16] {'depth'}, dimensions={0} | all-to-all | bytes 262144 | tf_op jit(solution)/shard_map/all_to_all | solution.py:334
  53.9 6.5 %middle.2 = (f32[128,16,128]{2,1,0:T(8,128)S(1)}, f32[128,16,128]{2,1,0:T(8,128)S(1)}, f32[128,16,128]{2,1,0:T(8,128)S(1)}, f32[128,16,128]{2,1,0:T(8,128)S(1)},...) custom-call(s32[3,128]{1,0:T(4,128)S(1)} %get-tuple-element.29.shift, ...), custom_call_target="tpu_custom_call" | custom-call | tf_op jit(solution)/shard_map/middle/pallas_call | solution.py:344
  60.5 8.5 %all_to_all.27.refs_3_ = f32[8,2,16,128]{3,2,1,0:T(8,128)S(1)} all-to-all(f32[8,2,16,128]{3,2,1,0:T(8,128)S(1)} %get-tuple-element.40), channel_id=1, replica_groups=mesh['depth'=8,'lat'=16] {'depth'}, dimensions={0} | all-to-all | bytes 262144 | tf_op jit(solution)/shard_map/all_to_all | solution.py:334
  69.0 7.3 %middle.3 = (f32[128,16,128]{2,1,0:T(8,128)S(1)}, f32[128,16,128]{2,1,0:T(8,128)S(1)}, f32[128,16,128]{2,1,0:T(8,128)S(1)}, f32[128,16,128]{2,1,0:T(8,128)S(1)},...) custom-call(s32[3,128]{1,0:T(4,128)S(1)} %get-tuple-element.29.shift, ...), custom_call_target="tpu_custom_call" | custom-call | tf_op jit(solution)/shard_map/middle/pallas_call | solution.py:344
  76.3 8.5 %all_to_all.28.refs_3_ = f32[8,2,16,128]{3,2,1,0:T(8,128)S(1)} all-to-all(f32[8,2,16,128]{3,2,1,0:T(8,128)S(1)} %get-tuple-element.48), channel_id=1, replica_groups=mesh['depth'=8,'lat'=16] {'depth'}, dimensions={0} | all-to-all | bytes 262144 | tf_op jit(solution)/shard_map/all_to_all | solution.py:334
  84.8 5.3 %last.1 = f32[16,256,128]{2,1,0:T(8,128)S(1)} custom-call(s32[3,128]{1,0:T(4,128)S(1)} %get-tuple-element.29.shift_ref.refs_0_, s32[3,128]{1,0:T(4,128)S(1)} %get-tuple-element.30.fraction_ref.refs_1_, f32[4,8]{1,0:T(4,128)S(1)} %get-tuple-element.31.table_ref.refs_2_, f32[8,2,16,128]{3,2,1,0:T(8,128)S(1)} %all_to_all.28.refs_3_, ...), custom_call_target="tpu_custom_call" | custom-call | tf_op jit(solution)/shard_map/last/pallas_call | solution.py:339
  90.1 31.3 %all_to_all.29.sent_ref = f32[16,256,128]{2,1,0:T(8,128)S(1)} all-to-all(f32[16,256,128]{2,1,0:T(8,128)S(1)} %last.1), channel_id=1, replica_groups=mesh['depth'=8,'lat'=16] {'lat'}, dimensions={0} | all-to-all | bytes 4194304 | tf_op jit(solution)/shard_map/all_to_all | solution.py:348
  121.4 1.4 %unpack.1 = (f32[128,16,128]{2,1,0:T(8,128)}, f32[128,16,128]{2,1,0:T(8,128)}) custom-call(f32[16,256,128]{2,1,0:T(8,128)S(1)} %all_to_all.29.sent_ref), custom_call_target="tpu_custom_call" | custom-call | tf_op jit(solution)/shard_map/unpack/pallas_call | solution.py:349

commit v3 on v2

--- a/solution.py
+++ b/solution.py
@@ -1,4 +1,5 @@
 import functools
+import math
 
 import jax
 import jax.numpy as jnp
@@ -13,12 +14,13 @@
 BETA_SECOND = 0.999
 ADAM_EPSILON = 0.001
 LOG2E = 1.4426950408889634
+TINY = 1e-37
 
 LANES = 128
 HALF = 8
 TOP = 8
 PADDED = 32
-GROUP = 16
+GROUP = 32
 CHUNKS = 4
 INTERPRET = False
 
@@ -61,27 +63,25 @@
     for age, old in enumerate(first):
         top = top + BETA_FIRST ** (age + 1) * old
         square = square + BETA_SECOND ** (age + 1) * (old * old)
-    top = top * (LEARN_RATE * (1.0 - BETA_FIRST) / (1.0 - BETA_FIRST**power))
-    square = square * ((1.0 - BETA_SECOND) / (1.0 - BETA_SECOND**power))
-    return top / (jnp.sqrt(square) + ADAM_EPSILON)
+    scale = math.sqrt((1.0 - BETA_SECOND) / (1.0 - BETA_SECOND**power))
+    rate = LEARN_RATE * (1.0 - BETA_FIRST) / (1.0 - BETA_FIRST**power) / scale
+    root = square * lax.rsqrt(jnp.maximum(square, TINY))
+    return rate * top / (root + ADAM_EPSILON / scale)
 
 
 def march(color, density, carry, planes):
-    depth, passing, light = carry
+    passing, light = carry
     density = density * LOG2E
     fade = jnp.exp2(-jnp.abs(density))
-    whole = 1.0 + fade
-    soft = jnp.maximum(density, 0.0) + (jnp.log2(whole) + (fade - (whole - 1.0)) * LOG2E)
+    soft = jnp.maximum(density, 0.0) + jnp.log2(1.0 + fade)
     slope = jnp.exp2(density - soft)
-    optical = soft * (1.0 / (planes * LOG2E))
-    series = optical * (1.0 - optical * (0.5 - optical * (1.0 / 6.0)))
-    opacity = jnp.where(optical < 0.01, series, 1.0 - jnp.exp2(soft * (-1.0 / planes)))
+    unit = 1.0 / (planes * LOG2E)
+    opacity = soft * (unit - soft * (unit**2 / 2.0 - soft * (unit**3 / 6.0)))
     blend = passing * opacity
-    depth = depth + soft
-    passing = jnp.exp2(depth * (-1.0 / planes))
+    passing = passing - blend
     light = light + blend * color
     reach = slope * (passing * color + light)
-    return (depth, passing, light), (blend, reach, slope)
+    return (passing, light), (blend, reach, slope)
 
 
 def clear_edges(buf):
@@ -98,7 +98,7 @@
 
 def fresh_carry():
     zero = jnp.zeros((HALF, LANES), jnp.float32)
-    return [(zero, zero + 1.0, zero) for _ in range(2)]
+    return [(zero + 1.0, zero) for _ in range(2)]
 
 
 def forward_group(view, base, buf, carry, scalars, outs, lane, planes):
@@ -118,7 +118,7 @@
 
 def put_slab(slab_ref, carry):
     for i in range(slab_ref.shape[0]):
-        put_halves(slab_ref, (i, 0), [carry[h][2] for h in range(2)])
+        put_halves(slab_ref, (i, 0), [carry[h][1] for h in range(2)])
         put_halves(slab_ref, (i, 1), [carry[h][0] for h in range(2)])
 
 
@@ -151,17 +151,15 @@
     found = []
     for h in range(2):
         rows = pl.ds(HALF * h, HALF)
-        depth = jnp.zeros((HALF, LANES), jnp.float32)
-        image = depth
-        front = depth
-        clear = depth + 1.0
-        passing = clear
+        image = jnp.zeros((HALF, LANES), jnp.float32)
+        front = image
+        passing = image + 1.0
+        clear = passing
         for i in range(slabs_ref.shape[0]):
             front = jnp.where(here == i, image, front)
             clear = jnp.where(here == i, passing, clear)
             image = image + passing * slabs_ref[i, 0, rows, :]
-            depth = depth + slabs_ref[i, 1, rows, :]
-            passing = jnp.exp2(depth * (-1.0 / planes))
+            passing = passing * slabs_ref[i, 1, rows, :]
         residual = image - goal_ref[view, rows, :]
         near = residual * clear
         found.append((near * planes, near, residual * (image - front)))

time: 123 us -> 120 us (0.976)
  Pallas kernels: 26.5 us -> 23.7 us
    pallas_call x2, Pallas kernels: 13.8 us -> 12.1 us  [body(): call(kernel, in_specs, [VMEM] * 8, [volume] * 7 + [slab], [padded, padded...]
where the time goes in v3:
time: 120 us
  blocking collectives  95.6 us (80%)
  Pallas kernels  23.7 us (20%)
    all_to_all x2, blocking collectives, body(): packed = lax.all_to_all(packed, 'lat', 0, 0, tiled=True)  68.2 us
    all_to_all x3, blocking collectives, body(): everyone = lax.all_to_all(sums, 'depth', 0, 0, tiled=True)  27.4 us
    pallas_call x2, Pallas kernels, body(): call(kernel, in_specs, [VMEM] * 8, [volume] * 7 + [slab], [padded, padded...  12.1 us
    pallas_call x1, Pallas kernels, body(): call(kernel, in_specs, VMEM, jax.ShapeDtypeStruct((tiles, 2 * depth_plane...  4.68 us
    pallas_call x1, Pallas kernels, body(): call(functools.partial(first_kernel, planes), [SMEM] * 3 + [VMEM], [VMEM]...  3.8 us

profile of v3, /device:TPU:0, one launch (start us, length us, event | category | flops | bytes accessed | tf_op | source)
XLA Modules:
  0.0 120.0 jit_solution(5091845540024119918)
XLA Ops:
  0.6 1.7 %pack.1 = (f32[16,264,128]{2,1,0:T(8,128)S(1)}, s32[3,128]{1,0:T(4,128)S(1)}, s32[3,128]{1,0:T(4,128)S(1)}, f32[4,8]{1,0:T(4,128)S(1)}) custom-call(f32[128,16,128]{2,1,0:T(8,128)} %e_ref.1, f32[128,16,128]{2,1,0:T(8,128)} %a_ref.1, f32[3,16,128]{2,1,0:T(8,128)} %goal_ref.1, s32[3,128]{1,0:T(4,128)} %shift_ref.1, s32[3,128]{1,0:T(4,128)} %fraction_ref.1, ...), custom_call_target="tpu_custom_call" | custom-call | tf_op jit(solution)/shard_map/pack/pallas_call | solution.py:319
  2.4 36.9 %all_to_all.25.sent_ref = f32[16,264,128]{2,1,0:T(8,128)S(1)} all-to-all(f32[16,264,128]{2,1,0:T(8,128)S(1)} %get-tuple-element.32), channel_id=1, replica_groups=mesh['depth'=8,'lat'=16] {'lat'}, dimensions={0} | all-to-all | bytes 4325376 | tf_op jit(solution)/shard_map/all_to_all | solution.py:325
  39.3 3.8 %first.1 = (f32[128,16,128]{2,1,0:T(8,128)S(1)}, f32[128,16,128]{2,1,0:T(8,128)S(1)}, f32[3,16,128]{2,1,0:T(8,128)S(1)}, f32[128,16,128]{2,1,0:T(8,128)S(1)}, f3...) custom-call(s32[3,128]{1,0:T(4,128)S(1)} %get-tuple-element.29.shift_ref.refs_0_, ...), custom_call_target="tpu_custom_call" | custom-call | tf_op jit(solution)/shard_map/first/pallas_call | solution.py:326
  43.1 10.4 %all_to_all.26.refs_3_ = f32[8,2,16,128]{3,2,1,0:T(8,128)S(1)} all-to-all(f32[8,2,16,128]{3,2,1,0:T(8,128)S(1)} %get-tuple-element.33), channel_id=1, replica_groups=mesh['depth'=8,'lat'=16] {'depth'}, dimensions={0} | all-to-all | bytes 262144 | tf_op jit(solution)/shard_map/all_to_all | solution.py:332
  53.5 6.0 %middle.2 = (f32[128,16,128]{2,1,0:T(8,128)S(1)}, f32[128,16,128]{2,1,0:T(8,128)S(1)}, f32[128,16,128]{2,1,0:T(8,128)S(1)}, f32[128,16,128]{2,1,0:T(8,128)S(1)},...) custom-call(s32[3,128]{1,0:T(4,128)S(1)} %get-tuple-element.29.shift, ...), custom_call_target="tpu_custom_call" | custom-call | tf_op jit(solution)/shard_map/middle/pallas_call | solution.py:342
  59.4 8.5 %all_to_all.27.refs_3_ = f32[8,2,16,128]{3,2,1,0:T(8,128)S(1)} all-to-all(f32[8,2,16,128]{3,2,1,0:T(8,128)S(1)} %get-tuple-element.40), channel_id=1, replica_groups=mesh['depth'=8,'lat'=16] {'depth'}, dimensions={0} | all-to-all | bytes 262144 | tf_op jit(solution)/shard_map/all_to_all | solution.py:332
  67.9 6.1 %middle.3 = (f32[128,16,128]{2,1,0:T(8,128)S(1)}, f32[128,16,128]{2,1,0:T(8,128)S(1)}, f32[128,16,128]{2,1,0:T(8,128)S(1)}, f32[128,16,128]{2,1,0:T(8,128)S(1)},...) custom-call(s32[3,128]{1,0:T(4,128)S(1)} %get-tuple-element.29.shift, ...), custom_call_target="tpu_custom_call" | custom-call | tf_op jit(solution)/shard_map/middle/pallas_call | solution.py:342
  74.1 8.5 %all_to_all.28.refs_3_ = f32[8,2,16,128]{3,2,1,0:T(8,128)S(1)} all-to-all(f32[8,2,16,128]{3,2,1,0:T(8,128)S(1)} %get-tuple-element.48), channel_id=1, replica_groups=mesh['depth'=8,'lat'=16] {'depth'}, dimensions={0} | all-to-all | bytes 262144 | tf_op jit(solution)/shard_map/all_to_all | solution.py:332
  82.6 4.7 %last.1 = f32[16,256,128]{2,1,0:T(8,128)S(1)} custom-call(s32[3,128]{1,0:T(4,128)S(1)} %get-tuple-element.29.shift_ref.refs_0_, s32[3,128]{1,0:T(4,128)S(1)} %get-tuple-element.30.fraction_ref.refs_1_, f32[4,8]{1,0:T(4,128)S(1)} %get-tuple-element.31.table_ref.refs_2_, f32[8,2,16,128]{3,2,1,0:T(8,128)S(1)} %all_to_all.28.refs_3_, ...), custom_call_target="tpu_custom_call" | custom-call | tf_op jit(solution)/shard_map/last/pallas_call | solution.py:337
  87.3 31.3 %all_to_all.29.sent_ref = f32[16,256,128]{2,1,0:T(8,128)S(1)} all-to-all(f32[16,256,128]{2,1,0:T(8,128)S(1)} %last.1), channel_id=1, replica_groups=mesh['depth'=8,'lat'=16] {'lat'}, dimensions={0} | all-to-all | bytes 4194304 | tf_op jit(solution)/shard_map/all_to_all | solution.py:346
  118.6 1.4 %unpack.1 = (f32[128,16,128]{2,1,0:T(8,128)}, f32[128,16,128]{2,1,0:T(8,128)}) custom-call(f32[16,256,128]{2,1,0:T(8,128)S(1)} %all_to_all.29.sent_ref), custom_call_target="tpu_custom_call" | custom-call | tf_op jit(solution)/shard_map/unpack/pallas_call | solution.py:347

commit v4 on v3

--- a/solution.py
+++ b/solution.py
@@ -20,7 +20,7 @@
 HALF = 8
 TOP = 8
 PADDED = 32
-GROUP = 32
+GROUP = 64
 CHUNKS = 4
 INTERPRET = False
 

time: 120 us -> 119 us (level)
  no operation moved by 1% of the time
where the time goes in v4:
time: 119 us
  blocking collectives  95.6 us (80%)
  Pallas kernels  22.7 us (19%)
    all_to_all x2, blocking collectives, body(): packed = lax.all_to_all(packed, 'lat', 0, 0, tiled=True)  68.2 us
    all_to_all x3, blocking collectives, body(): everyone = lax.all_to_all(sums, 'depth', 0, 0, tiled=True)  27.3 us
    pallas_call x2, Pallas kernels, body(): call(kernel, in_specs, [VMEM] * 8, [volume] * 7 + [slab], [padded, padded...  11.7 us
    pallas_call x1, Pallas kernels, body(): call(kernel, in_specs, VMEM, jax.ShapeDtypeStruct((tiles, 2 * depth_plane...  4.19 us
    pallas_call x1, Pallas kernels, body(): call(functools.partial(first_kernel, planes), [SMEM] * 3 + [VMEM], [VMEM]...  3.65 us

profile of v4, /device:TPU:0, one launch (start us, length us, event | category | flops | bytes accessed | tf_op | source)
XLA Modules:
  0.0 119.0 jit_solution(9513401246601141795)
XLA Ops:
  0.6 1.7 %pack.1 = (f32[16,264,128]{2,1,0:T(8,128)S(1)}, s32[3,128]{1,0:T(4,128)S(1)}, s32[3,128]{1,0:T(4,128)S(1)}, f32[4,8]{1,0:T(4,128)S(1)}) custom-call(f32[128,16,128]{2,1,0:T(8,128)} %e_ref.1, f32[128,16,128]{2,1,0:T(8,128)} %a_ref.1, f32[3,16,128]{2,1,0:T(8,128)} %goal_ref.1, s32[3,128]{1,0:T(4,128)} %shift_ref.1, s32[3,128]{1,0:T(4,128)} %fraction_ref.1, ...), custom_call_target="tpu_custom_call" | custom-call | tf_op jit(solution)/shard_map/pack/pallas_call | solution.py:319
  2.4 36.9 %all_to_all.25.sent_ref = f32[16,264,128]{2,1,0:T(8,128)S(1)} all-to-all(f32[16,264,128]{2,1,0:T(8,128)S(1)} %get-tuple-element.32), channel_id=1, replica_groups=mesh['depth'=8,'lat'=16] {'lat'}, dimensions={0} | all-to-all | bytes 4325376 | tf_op jit(solution)/shard_map/all_to_all | solution.py:325
  39.3 3.7 %first.1 = (f32[128,16,128]{2,1,0:T(8,128)S(1)}, f32[128,16,128]{2,1,0:T(8,128)S(1)}, f32[3,16,128]{2,1,0:T(8,128)S(1)}, f32[128,16,128]{2,1,0:T(8,128)S(1)}, f3...) custom-call(s32[3,128]{1,0:T(4,128)S(1)} %get-tuple-element.29.shift_ref.refs_0_, ...), custom_call_target="tpu_custom_call" | custom-call | tf_op jit(solution)/shard_map/first/pallas_call | solution.py:326
  42.9 10.4 %all_to_all.26.refs_3_ = f32[8,2,16,128]{3,2,1,0:T(8,128)S(1)} all-to-all(f32[8,2,16,128]{3,2,1,0:T(8,128)S(1)} %get-tuple-element.33), channel_id=1, replica_groups=mesh['depth'=8,'lat'=16] {'depth'}, dimensions={0} | all-to-all | bytes 262144 | tf_op jit(solution)/shard_map/all_to_all | solution.py:332
  53.3 5.8 %middle.2 = (f32[128,16,128]{2,1,0:T(8,128)S(1)}, f32[128,16,128]{2,1,0:T(8,128)S(1)}, f32[128,16,128]{2,1,0:T(8,128)S(1)}, f32[128,16,128]{2,1,0:T(8,128)S(1)},...) custom-call(s32[3,128]{1,0:T(4,128)S(1)} %get-tuple-element.29.shift, ...), custom_call_target="tpu_custom_call" | custom-call | tf_op jit(solution)/shard_map/middle/pallas_call | solution.py:342
  59.1 8.5 %all_to_all.27.refs_3_ = f32[8,2,16,128]{3,2,1,0:T(8,128)S(1)} all-to-all(f32[8,2,16,128]{3,2,1,0:T(8,128)S(1)} %get-tuple-element.40), channel_id=1, replica_groups=mesh['depth'=8,'lat'=16] {'depth'}, dimensions={0} | all-to-all | bytes 262144 | tf_op jit(solution)/shard_map/all_to_all | solution.py:332
  67.5 6.0 %middle.3 = (f32[128,16,128]{2,1,0:T(8,128)S(1)}, f32[128,16,128]{2,1,0:T(8,128)S(1)}, f32[128,16,128]{2,1,0:T(8,128)S(1)}, f32[128,16,128]{2,1,0:T(8,128)S(1)},...) custom-call(s32[3,128]{1,0:T(4,128)S(1)} %get-tuple-element.29.shift, ...), custom_call_target="tpu_custom_call" | custom-call | tf_op jit(solution)/shard_map/middle/pallas_call | solution.py:342
  73.5 8.5 %all_to_all.28.refs_3_ = f32[8,2,16,128]{3,2,1,0:T(8,128)S(1)} all-to-all(f32[8,2,16,128]{3,2,1,0:T(8,128)S(1)} %get-tuple-element.48), channel_id=1, replica_groups=mesh['depth'=8,'lat'=16] {'depth'}, dimensions={0} | all-to-all | bytes 262144 | tf_op jit(solution)/shard_map/all_to_all | solution.py:332
  82.0 4.2 %last.1 = f32[16,256,128]{2,1,0:T(8,128)S(1)} custom-call(s32[3,128]{1,0:T(4,128)S(1)} %get-tuple-element.29.shift_ref.refs_0_, s32[3,128]{1,0:T(4,128)S(1)} %get-tuple-element.30.fraction_ref.refs_1_, f32[4,8]{1,0:T(4,128)S(1)} %get-tuple-element.31.table_ref.refs_2_, f32[8,2,16,128]{3,2,1,0:T(8,128)S(1)} %all_to_all.28.refs_3_, ...), custom_call_target="tpu_custom_call" | custom-call | tf_op jit(solution)/shard_map/last/pallas_call | solution.py:337
  86.2 31.3 %all_to_all.29.sent_ref = f32[16,256,128]{2,1,0:T(8,128)S(1)} all-to-all(f32[16,256,128]{2,1,0:T(8,128)S(1)} %last.1), channel_id=1, replica_groups=mesh['depth'=8,'lat'=16] {'lat'}, dimensions={0} | all-to-all | bytes 4194304 | tf_op jit(solution)/shard_map/all_to_all | solution.py:346
  117.5 1.4 %unpack.1 = (f32[128,16,128]{2,1,0:T(8,128)}, f32[128,16,128]{2,1,0:T(8,128)}) custom-call(f32[16,256,128]{2,1,0:T(8,128)S(1)} %all_to_all.29.sent_ref), custom_call_target="tpu_custom_call" | custom-call | tf_op jit(solution)/shard_map/unpack/pallas_call | solution.py:347

commit v5 on v4

--- a/solution.py
+++ b/solution.py
@@ -57,16 +57,14 @@
 def adam_change(view, grad, first):
     power = view + 1
     if view == 0:
-        return LEARN_RATE * grad / (jnp.abs(grad) + ADAM_EPSILON)
-    top = grad
-    square = grad * grad
-    for age, old in enumerate(first):
-        top = top + BETA_FIRST ** (age + 1) * old
-        square = square + BETA_SECOND ** (age + 1) * (old * old)
+        return LEARN_RATE * grad / (jnp.abs(grad) + ADAM_EPSILON), (grad,)
+    old_top, old_square = (first[0], first[0] * first[0]) if view == 1 else first
+    top = BETA_FIRST * old_top + grad
+    square = BETA_SECOND * old_square + grad * grad
     scale = math.sqrt((1.0 - BETA_SECOND) / (1.0 - BETA_SECOND**power))
     rate = LEARN_RATE * (1.0 - BETA_FIRST) / (1.0 - BETA_FIRST**power) / scale
     root = square * lax.rsqrt(jnp.maximum(square, TINY))
-    return rate * top / (root + ADAM_EPSILON / scale)
+    return rate * top / (root + ADAM_EPSILON / scale), (top, square)
 
 
 def march(color, density, carry, planes):
@@ -177,13 +175,13 @@
 
     shift_ref, fraction_ref, table_ref, slabs_ref, goal_ref = take(5)
     fields = take(2)
-    old = [take(2) for _ in range(view)][::-1]
+    old = [take(2) for _ in range(view)]
     kept = take(3)
     if last:
         (sent_ref,) = take(1)
         gbuf, fbuf = refs
     else:
-        new_fields, grads, new_kept, (slab_ref,) = take(2), take(2), take(3), take(1)
+        new_fields, states, new_kept, (slab_ref,) = take(2), [take(2) for _ in range(view + 1)], take(3), take(1)
         gbuf, fbuf = refs
         clear_edges(fbuf)
     clear_edges(gbuf)
@@ -209,11 +207,13 @@
                 for h in range(2):
                     rows = pl.ds(HALF * h, HALF)
                     first = [pair[f][z, rows, :] for pair in old]
-                    value = fields[f][z, rows, :] - adam_change(view, grad[h], first)
+                    change, state = adam_change(view, grad[h], first)
+                    value = fields[f][z, rows, :] - change
                     fbuf[p, f, pl.ds(TOP + HALF * h, HALF), :] = value
                     if not last:
                         new_fields[f][z, rows, :] = value
-                        grads[f][z, rows, :] = grad[h]
+                        for pair, moment in zip(states, state):
+                            pair[f][z, rows, :] = moment
         if last:
             for f in range(2):
                 for g in range(GROUP // HALF):
@@ -339,10 +339,12 @@
                 jax.ShapeDtypeStruct((tiles, 2 * depth_planes, width), jnp.float32), [padded, padded], "last",
             )(*operands)
         else:
-            e, a, g_e, g_a, *kept, sums = call(
-                kernel, in_specs, [VMEM] * 8, [volume] * 7 + [slab], [padded, padded], "middle",
+            moments = 2 * (view + 1)
+            e, a, *rest, sums = call(
+                kernel, in_specs, [VMEM] * (moments + 6), [volume] * (moments + 5) + [slab],
+                [padded, padded], "middle",
             )(*operands)
-            old = [*old, g_e, g_a]
+            old, kept = rest[:moments], rest[moments:]
     packed = lax.all_to_all(packed, "lat", 0, 0, tiled=True)
     return call(
         unpack_kernel, [VMEM], [HBM, HBM], [volume, volume], [store, store, sems], "unpack")(packed)

time: 119 us -> 119 us (level)
  no operation moved by 1% of the time
where the time goes in v5:
time: 119 us
  blocking collectives  95.6 us (80%)
  Pallas kernels  22.6 us (19%)
    all_to_all x2, blocking collectives, body(): packed = lax.all_to_all(packed, 'lat', 0, 0, tiled=True)  68.2 us
    all_to_all x3, blocking collectives, body(): everyone = lax.all_to_all(sums, 'depth', 0, 0, tiled=True)  27.3 us
    pallas_call x2, Pallas kernels, body(): call(kernel, in_specs, [VMEM] * (moments + 6), [volume] * (moments + 5) +...  11.8 us
    pallas_call x1, Pallas kernels, body(): call(kernel, in_specs, VMEM, jax.ShapeDtypeStruct((tiles, 2 * depth_plane...  3.99 us
    pallas_call x1, Pallas kernels, body(): call(functools.partial(first_kernel, planes), [SMEM] * 3 + [VMEM], [VMEM]...  3.65 us

profile of v5, /device:TPU:0, one launch (start us, length us, event | category | flops | bytes accessed | tf_op | source)
XLA Modules:
  0.0 118.9 jit_solution(8405827073572364810)
XLA Ops:
  0.6 1.7 %pack.1 = (f32[16,264,128]{2,1,0:T(8,128)S(1)}, s32[3,128]{1,0:T(4,128)S(1)}, s32[3,128]{1,0:T(4,128)S(1)}, f32[4,8]{1,0:T(4,128)S(1)}) custom-call(f32[128,16,128]{2,1,0:T(8,128)} %e_ref.1, f32[128,16,128]{2,1,0:T(8,128)} %a_ref.1, f32[3,16,128]{2,1,0:T(8,128)} %goal_ref.1, s32[3,128]{1,0:T(4,128)} %shift_ref.1, s32[3,128]{1,0:T(4,128)} %fraction_ref.1, ...), custom_call_target="tpu_custom_call" | custom-call | tf_op jit(solution)/shard_map/pack/pallas_call | solution.py:319
  2.4 36.9 %all_to_all.25.sent_ref = f32[16,264,128]{2,1,0:T(8,128)S(1)} all-to-all(f32[16,264,128]{2,1,0:T(8,128)S(1)} %get-tuple-element.34), channel_id=1, replica_groups=mesh['depth'=8,'lat'=16] {'lat'}, dimensions={0} | all-to-all | bytes 4325376 | tf_op jit(solution)/shard_map/all_to_all | solution.py:325
  39.3 3.7 %first.1 = (f32[128,16,128]{2,1,0:T(8,128)S(1)}, f32[128,16,128]{2,1,0:T(8,128)S(1)}, f32[3,16,128]{2,1,0:T(8,128)S(1)}, f32[128,16,128]{2,1,0:T(8,128)S(1)}, f3...) custom-call(s32[3,128]{1,0:T(4,128)S(1)} %get-tuple-element.31.shift_ref.refs_0_, ...), custom_call_target="tpu_custom_call" | custom-call | tf_op jit(solution)/shard_map/first/pallas_call | solution.py:326
  42.9 10.4 %all_to_all.26.refs_3_ = f32[8,2,16,128]{3,2,1,0:T(8,128)S(1)} all-to-all(f32[8,2,16,128]{3,2,1,0:T(8,128)S(1)} %get-tuple-element.35), channel_id=1, replica_groups=mesh['depth'=8,'lat'=16] {'depth'}, dimensions={0} | all-to-all | bytes 262144 | tf_op jit(solution)/shard_map/all_to_all | solution.py:332
  53.3 5.8 %middle.2 = (f32[128,16,128]{2,1,0:T(8,128)S(1)}, f32[128,16,128]{2,1,0:T(8,128)S(1)}, f32[128,16,128]{2,1,0:T(8,128)S(1)}, f32[128,16,128]{2,1,0:T(8,128)S(1)},...) custom-call(s32[3,128]{1,0:T(4,128)S(1)} %get-tuple-element.31.shift, ...), custom_call_target="tpu_custom_call" | custom-call | tf_op jit(solution)/shard_map/middle/pallas_call | solution.py:343
  59.0 8.5 %all_to_all.27.refs_3_ = f32[8,2,16,128]{3,2,1,0:T(8,128)S(1)} all-to-all(f32[8,2,16,128]{3,2,1,0:T(8,128)S(1)} %get-tuple-element.42), channel_id=1, replica_groups=mesh['depth'=8,'lat'=16] {'depth'}, dimensions={0} | all-to-all | bytes 262144 | tf_op jit(solution)/shard_map/all_to_all | solution.py:332
  67.5 6.1 %middle.3 = (f32[128,16,128]{2,1,0:T(8,128)S(1)}, f32[128,16,128]{2,1,0:T(8,128)S(1)}, f32[128,16,128]{2,1,0:T(8,128)S(1)}, f32[128,16,128]{2,1,0:T(8,128)S(1)},...) custom-call(s32[3,128]{1,0:T(4,128)S(1)} %get-tuple-element.31.shift, ...), custom_call_target="tpu_custom_call" | custom-call | tf_op jit(solution)/shard_map/middle/pallas_call | solution.py:343
  73.6 8.5 %all_to_all.28.refs_3_ = f32[8,2,16,128]{3,2,1,0:T(8,128)S(1)} all-to-all(f32[8,2,16,128]{3,2,1,0:T(8,128)S(1)} %get-tuple-element.50), channel_id=1, replica_groups=mesh['depth'=8,'lat'=16] {'depth'}, dimensions={0} | all-to-all | bytes 262144 | tf_op jit(solution)/shard_map/all_to_all | solution.py:332
  82.1 4.0 %last.1 = f32[16,256,128]{2,1,0:T(8,128)S(1)} custom-call(s32[3,128]{1,0:T(4,128)S(1)} %get-tuple-element.31.shift_ref.refs_0_, s32[3,128]{1,0:T(4,128)S(1)} %get-tuple-element.32.fraction_ref.refs_1_, f32[4,8]{1,0:T(4,128)S(1)} %get-tuple-element.33.table_ref.refs_2_, f32[8,2,16,128]{3,2,1,0:T(8,128)S(1)} %all_to_all.28.refs_3_, ...), custom_call_target="tpu_custom_call" | custom-call | tf_op jit(solution)/shard_map/last/pallas_call | solution.py:337
  86.1 31.3 %all_to_all.29.sent_ref = f32[16,256,128]{2,1,0:T(8,128)S(1)} all-to-all(f32[16,256,128]{2,1,0:T(8,128)S(1)} %last.1), channel_id=1, replica_groups=mesh['depth'=8,'lat'=16] {'lat'}, dimensions={0} | all-to-all | bytes 4194304 | tf_op jit(solution)/shard_map/all_to_all | solution.py:348
  117.4 1.4 %unpack.1 = (f32[128,16,128]{2,1,0:T(8,128)}, f32[128,16,128]{2,1,0:T(8,128)}) custom-call(f32[16,256,128]{2,1,0:T(8,128)S(1)} %all_to_all.29.sent_ref), custom_call_target="tpu_custom_call" | custom-call | tf_op jit(solution)/shard_map/unpack/pallas_call | solution.py:349
